TPU v7x, 1024 devices: a whole 4x8x16 slice. The times are simulated.
1024 devices in a mesh: lev: 2 (over core), lat: 32 (over y, z_hi), lon: 16 (over z_lo, x).
Axes of the slice: x: 4, y: 8, z: 16 (z_hi: 4, z_lo: 4; z = z_hi * 4 + z_lo), core: 2. Of those that a mesh axis runs over, the one named last changes fastest.
Arguments:
- grid: bfloat16 [4, 192, 384, 512], P('lev', 'lat', 'lon'), may hold values from -12 to 12
- w_qkv: bfloat16 [512, 1536], replicated, may hold values from -0.25 to 0.25
- w_proj: bfloat16 [512, 512], replicated, may hold values from -0.25 to 0.25
- w_up: bfloat16 [512, 2048], replicated, may hold values from -0.25 to 0.25
- w_down: bfloat16 [2048, 512], replicated, may hold values from -0.125 to 0.125
- logit_scale: float32 [8], replicated, may hold values from 3 to 24
- gain_attn: float32 [512], replicated, may hold values from 0.1 to 1.9
- gain_mlp: float32 [512], replicated, may hold values from 0.1 to 1.9
Outputs:
- updated: bfloat16 [4, 192, 384, 512], P('lev', 'lat', 'lon')
All inputs are finite; a program needn't handle non-finite values.
Results may differ from a plain program's by a relative error of at most 0.01.
Values may be sent and summed in bfloat16 or wider, within the bound.
No kernel may reach another device: no remote copies, remote signals or barrier semaphores. Data moves between devices by JAX's collectives and lax.ppermute only.
A program may use at most 32 MiB of HBM per device.

v0:
```python
import jax
import jax.numpy as jnp
from jax import lax
from jax.sharding import PartitionSpec as P

WA = 6
WO = 12


def from_partner(block, axis, bit):
    count = lax.axis_size(axis)
    route = []
    for low in range(count):
        high = low | 1 << bit
        if high != low and high < count:
            route += [(low, high), (high, low)]
    return lax.ppermute(block, axis, route)


def from_behind(array, axis, by):
    length = lax.axis_size(axis)
    return lax.ppermute(array, axis, [(i, (i + by) % length) for i in range(length)])


def layer_norm(values, gain):
    mean = jnp.mean(values, axis=-1, keepdims=True)
    centred = values - mean
    spread = jnp.mean(centred * centred, axis=-1, keepdims=True)
    return centred * lax.rsqrt(spread + 1e-05) * gain


def to_windows(values, depth):
    levels, rows, cols, width = values.shape
    shaped = values.reshape(levels // depth, depth, rows // WA, WA, cols // WO, WO, width)
    shaped = jnp.transpose(shaped, (0, 2, 4, 1, 3, 5, 6))
    return shaped.reshape(-1, depth * WA * WO, width)


def from_windows(values, depth, levels, rows, cols):
    width = values.shape[-1]
    shaped = values.reshape(levels // depth, rows // WA, cols // WO, depth, WA, WO, width)
    shaped = jnp.transpose(shaped, (0, 3, 1, 4, 2, 5, 6))
    return shaped.reshape(levels, rows, cols, width)


def attend(packed, region, logit_scale):
    count, span, triple = packed.shape
    width = triple // 3
    heads = logit_scale.shape[0]
    size = width // heads
    query = packed[..., :width].reshape(count, span, heads, size)
    keys = packed[..., width : 2 * width].reshape(count, span, heads, size)
    values = packed[..., 2 * width :].reshape(count, span, heads, size)
    raw = jnp.einsum("bqhd,bkhd->bhqk", query, keys, preferred_element_type=jnp.float32)
    query_f = query.astype(jnp.float32)
    keys_f = keys.astype(jnp.float32)
    q_scale = lax.rsqrt(jnp.sum(query_f * query_f, axis=-1) + 1e-06)
    k_scale = lax.rsqrt(jnp.sum(keys_f * keys_f, axis=-1) + 1e-06)
    scores = raw * logit_scale[None, :, None, None]
    scores = scores * jnp.transpose(q_scale, (0, 2, 1))[:, :, :, None]
    scores = scores * jnp.transpose(k_scale, (0, 2, 1))[:, :, None, :]
    same = region[:, None, :, None] == region[:, None, None, :]
    expd = jnp.where(same, jnp.exp(scores), jnp.zeros_like(scores))
    weights = (expd / jnp.sum(expd, axis=-1, keepdims=True)).astype(jnp.bfloat16)
    mixed = jnp.einsum("bhqk,bkhd->bqhd", weights, values, preferred_element_type=jnp.float32)
    return mixed.astype(jnp.bfloat16).reshape(count, span, width)


def per_device(grid, w_qkv, w_proj, w_up, w_down, logit_scale, gain_attn, gain_mlp):
    levels, rows, cols, width = grid.shape
    half_rows = WA // 2
    half_cols = WO // 2
    lev_index = lax.axis_index("lev")
    lat_index = lax.axis_index("lat")
    all_rows = rows * lax.axis_size("lat")
    level_global = lev_index + jnp.arange(levels + 1, dtype=jnp.int32)
    level_region = (level_global + 1) // 2
    lat_global = (lat_index * rows + half_rows + jnp.arange(rows, dtype=jnp.int32)) % all_rows
    lat_region = (lat_global >= half_rows).astype(jnp.int32)
    region = (
        level_region[:, None, None] * 2
        + lat_region[None, :, None]
        + jnp.zeros((levels + 1, rows, cols), jnp.int32)
    )
    region_windows = to_windows(region[..., None], levels + 1)[..., 0]
    inner = jnp.where(lev_index == 0, grid[1:2], grid[0:1])
    partner = from_partner(inner, "lev", 0)
    stacked = jnp.where(
        lev_index == 0, jnp.concatenate([grid, partner], 0), jnp.concatenate([partner, grid], 0)
    )
    lat_head = from_behind(stacked[:, :half_rows], "lat", -1)
    lon_head = from_behind(stacked[:, :, :half_cols], "lon", -1)
    corner_piece = from_behind(lon_head[:, :half_rows], "lat", -1)
    row_moved = jnp.concatenate([stacked[:, half_rows:], lat_head], 1)
    right_side = jnp.concatenate([lon_head[:, half_rows:], corner_piece], 1)
    moved = jnp.concatenate([row_moved[:, :, half_cols:], right_side], 2)
    packed = jnp.dot(moved.reshape(-1, width), w_qkv, preferred_element_type=jnp.float32).astype(
        jnp.bfloat16
    )
    windowed_packed = packed.reshape(levels + 1, rows, cols, 3 * width)
    windows = to_windows(windowed_packed, levels + 1)
    mixed = attend(windows, region_windows, logit_scale)
    mixed = from_windows(mixed, levels + 1, levels + 1, rows, cols)
    own = lax.dynamic_slice_in_dim(mixed, lev_index, levels, 0)
    attn_out = jnp.dot(own.reshape(-1, width), w_proj, preferred_element_type=jnp.float32)
    attn_out = attn_out.astype(jnp.bfloat16).reshape(levels, rows, cols, width)
    own_stream = lax.dynamic_slice_in_dim(moved, lev_index, levels, 0)
    total = own_stream.astype(jnp.float32) + layer_norm(attn_out.astype(jnp.float32), gain_attn)
    flat = total.astype(jnp.bfloat16).reshape(-1, width)
    hidden = jax.nn.gelu(
        jnp.dot(flat, w_up, preferred_element_type=jnp.float32), approximate=True
    ).astype(jnp.bfloat16)
    down = jnp.dot(hidden, w_down, preferred_element_type=jnp.float32)
    result = (flat.astype(jnp.float32) + layer_norm(down, gain_mlp)).astype(jnp.bfloat16)
    values = result.reshape(levels, rows, cols, width)
    tail_cols = from_behind(values[:, :, cols - half_cols :], "lon", 1)
    values = jnp.concatenate([tail_cols, values[:, :, : cols - half_cols]], 2)
    tail_rows = from_behind(values[:, rows - half_rows :], "lat", 1)
    return jnp.concatenate([tail_rows, values[:, : rows - half_rows]], 1)


def solution(mesh):
    placed = (P("lev", "lat", "lon", None), P(), P(), P(), P(), P(), P(), P())
    return jax.shard_map(
        per_device,
        mesh=mesh,
        in_specs=placed,
        out_specs=P("lev", "lat", "lon", None),
        check_vma=False,
    )
```

profile of v0, /device:TPU:1, one launch (start us, length us, event | category | flops | bytes accessed | tf_op | source)
XLA Modules:
  0.0 113.0 jit_solution(5008521930430639391)
XLA Ops:
  0.0 1.1 %slice_select_fusion = bf16[1,6,24,512]{3,2,1,0:T(8,128)(2,1)S(1)} fusion(bf16[2,6,24,512]{3,2,1,0:T(8,128)(2,1)} %param.8, pred[]{:T(512)S(6)} %eq.24), kind=kLoop, calls=%fused_computation.34 | loop fusion | flops 73728 | bytes 442369 | tf_op jit(solution)/shard_map/jit(_where)/select_n | solution.py:86
  1.2 16.0 %collective-permute-start = (bf16[1,6,24,512]{3,2,1,0:T(8,128)(2,1)S(1)}, bf16[1,6,24,512]{3,2,1,0:T(8,128)(2,1)S(1)}, u32[]{:S(2)}, u32[]{:S(2)}) collective-permute-start(bf16[1,6,24,512]{3,2,1,0:T(8,128)(2,1)S(1)} %slice_select_fusion), channel_id=1, source_target_pairs={{0,512},{512,0},{1,513},{513,1},{2,514},{514,2},{3,515},{515,3},{4... | collective-permute-start | bytes 442376 | tf_op jit(solution)/shard_map/ppermute | solution.py:17
  17.2 0.1 broadcast_add_fusion
  17.3 0.1 transpose.50
  17.4 0.1 transpose.51
  17.5 0.7 collective-permute-done
  18.2 1.1 maximum_select_fusion
  19.3 1.9 %collective-permute-start.2 = (bf16[3,6,6,512]{3,2,1,0:T(8,128)(2,1)S(1)}, bf16[3,6,6,512]{3,2,1,0:T(8,128)(2,1)S(1)}, u32[]{:S(2)}, u32[]{:S(2)}) collective-permute-start(bf16[3,6,6,512]{3,2,1,0:T(8,128)(2,1)S(1)} %slice.62), channel_id=1, source_target_pairs={{0,15},{1,0},{2,1},{3,2},{4,3},{5,4},{6,5},{7,6},{8,7},{9,8},{10,9... | collective-permute-start | bytes 331784 | tf_op jit(solution)/shard_map/ppermute | solution.py:22
  21.3 13.4 %collective-permute-start.1 = (bf16[3,3,24,512]{3,2,1,0:T(8,128)(2,1)S(1)}, bf16[3,3,24,512]{3,2,1,0:T(8,128)(2,1)S(1)}, u32[]{:S(2)}, u32[]{:S(2)}) collective-permute-start(bf16[3,3,24,512]{3,2,1,0:T(8,128)(2,1)S(1)} %get-tuple-element.9), channel_id=1, source_target_pairs={{0,496},{16,0},{32,16},{48,32},{64,48},{80,64},{96,80},{112,96},{1... | collective-permute-start | bytes 663560 | tf_op jit(solution)/shard_map/ppermute | solution.py:22
  34.7 0.0 collective-permute-done.2
  34.7 3.4 %collective-permute-start.3 = (bf16[3,3,6,512]{3,2,1,0:T(8,128)(2,1)S(1)}, bf16[3,3,6,512]{3,2,1,0:T(8,128)(2,1)S(1)}, u32[]{:S(2)}, u32[]{:S(2)}) collective-permute-start(bf16[3,3,6,512]{3,2,1,0:T(8,128)(2,1)S(1)} %get-tuple-element.11), channel_id=1, source_target_pairs={{0,496},{16,0},{32,16},{48,32},{64,48},{80,64},{96,80},{112,96},{1... | collective-permute-start | bytes 165896 | tf_op jit(solution)/shard_map/ppermute | solution.py:22
  38.1 0.1 broadcast_compare_fusion
  38.2 11.5 %collective-permute-done.3 = bf16[3,3,6,512]{3,2,1,0:T(8,128)(2,1)S(1)} collective-permute-done((bf16[3,3,6,512]{3,2,1,0:T(8,128)(2,1)S(1)}, bf16[3,3,6,512]{3,2,1,0:T(8,128)(2,1)S(1)}, u32[]{:S(2)}, u32[]{:S(2)}) %collective-permute-start.3) | collective-permute-done | bytes 55328 | tf_op jit(solution)/shard_map/ppermute | solution.py:22
  49.7 0.0 collective-permute-done.1
  49.7 0.2 fusion.15
  49.9 0.8 copy-done.1
  50.6 2.3 %convolution_convert_fusion = bf16[432,1536]{1,0:T(8,128)(2,1)S(1)} fusion(bf16[432,512]{1,0:T(8,128)(2,1)S(1)} %bitcast.46, bf16[512,1536]{1,0:T(8,128)(2,1)} %param.9), kind=kOutput, calls=%fused_computation.3 | convolution fusion | flops 680140800 | bytes 3342336 | tf_op jit(solution)/shard_map/dot_general | solution.py:97
  52.9 1.4 %reshape_reshape.6 = bf16[1,3,1,6,2,12,1536]{6,5,4,3,1,2,0:T(8,128)(2,1)} reshape(bf16[432,1536]{1,0:T(8,128)(2,1)S(1)} %convolution_convert_fusion) | data formatting | bytes 2654208 | tf_op jit(solution)/shard_map/reshape;reshape | solution.py:34
  54.3 2.8 %copy.10 = bf16[1,1,2,3,6,12,1536]{6,2,5,4,3,1,0:T(2,128)(2,1)S(1)} copy(bf16[1,1,2,3,6,12,1536]{6,5,2,4,3,1,0:T(8,128)(2,1)} %bitcast.37) | data formatting | bytes 2654208 | tf_op jit(solution)/shard_map/transpose | solution.py:35
  57.1 1.8 %fusion.24 = (bf16[2,216,512]{2,0,1:T(2,128)(2,1)S(1)}, bf16[2,216,512]{2,0,1:T(2,128)(2,1)}, bf16[2,216,512]{2,0,1:T(2,128)(2,1)}) fusion(bf16[2,216,1536]{2,0,1:T(2,128)(2,1)S(1)} %bitcast.39), kind=kLoop, calls=%fused_computation.55 | loop fusion | bytes 2654208 | tf_op jit(solution)/shard_map/slice | solution.py:52
  59.0 0.5 copy.13
  59.5 0.1 multiply_reduce_fusion
  59.6 1.3 %copy.12 = bf16[2,216,512]{1,2,0:T(8,128)(2,1)S(1)} copy(bf16[2,216,512]{2,0,1:T(2,128)(2,1)} %get-tuple-element.6) | data formatting | bytes 884736 | tf_op jit(solution)/shard_map/slice | solution.py:51
  60.9 0.1 multiply_reduce_fusion.1
  61.1 2.0 %copy.11 = bf16[2,216,512]{1,2,0:T(8,128)(2,1)} copy(bf16[2,216,512]{2,0,1:T(2,128)(2,1)} %get-tuple-element.7) | data formatting | bytes 884736 | tf_op jit(solution)/shard_map/slice | solution.py:53
  63.1 1.5 %fusion = (f32[2,8,216]{2,1,0:T(8,128)S(1)}, f32[2,8,216,216]{2,3,1,0:T(8,128)S(1)}) fusion(f32[2,8,216]{2,1,0:T(8,128)S(1)} %get-tuple-element.18, f32[2,8,216]{2,1,0:T(8,128)S(1)} %get-tuple-element.19, f32[8]{0:T(128)S(1)} %copy-done.6, pred[2,216,216]{1,2,0:T(8,128)(4,1)S(1)} %broadcast_compare_fusion, bf16[2,216,8,64]{1,3,2,0:T(8,128)(2,1)S(1)} %bitcast.44, ...), kind=kOutput, calls=%fused_computation.4 | convolution fusion | flops 99280512 | bytes 4005536 | tf_op jit(solution)/shard_map/bqhd,bkhd->bhqk/dot_general | solution.py:54
  64.6 2.2 %fusion.11 = bf16[2,216,8,64]{1,3,2,0:T(8,128)(2,1)} fusion(bf16[2,216,8,64]{1,3,2,0:T(8,128)(2,1)S(1)} %bitcast.49, f32[2,8,216,216]{2,3,1,0:T(8,128)S(1)} %get-tuple-element.13, f32[2,8,216]{2,1,0:T(8,128)S(1)} %get-tuple-element.12, f32[2,8,216]{2,1,0:T(8,128)S(1)} %get-tuple-element.18, f32[2,8,216]{2,1,0:T(8,128)S(1)} %get-tuple-element.19, ...), kind=kOutput, calls=%fused_computation.15 | convolution fusion | flops 100251648 | bytes 4005536 | tf_op jit(solution)/shard_map/bhqk,bkhd->bqhd/dot_general | solution.py:65
  66.8 1.8 %copy.15 = bf16[2,216,8,64]{3,2,0,1:T(8,128)(2,1)S(1)} copy(bf16[2,216,8,64]{1,3,2,0:T(8,128)(2,1)} %fusion.11) | data formatting | bytes 884736 | tf_op jit(solution)/shard_map/convert_element_type | solution.py:66
  68.6 0.4 reshape_reshape.7
  69.0 0.0 copy-start.4
  69.0 0.1 copy.16
  69.1 0.1 reshape.154
  69.3 1.5 %fusion.27 = (f32[288]{0:T(512)S(1)}, f32[288,512]{1,0:T(8,128)S(1)}) fusion(bf16[288,512]{1,0:T(8,128)(2,1)S(1)} %bitcast.47, bf16[512,512]{1,0:T(8,128)(2,1)} %param.10), kind=kOutput, calls=%fused_computation.58 | convolution fusion | flops 151437024 | bytes 1410176 | tf_op jit(solution)/shard_map/dot_general | solution.py:105
  70.8 0.1 div.38
  70.9 0.2 multiply_reduce_fusion.3
  71.1 0.1 rsqrt.38
  71.2 0.0 copy-done.4
  71.3 0.2 add_convert_fusion.1
  71.5 0.0 copy-start.5
  71.5 3.4 %fusion.28 = (f32[288]{0:T(512)S(1)}, f32[288,512]{1,0:T(8,128)S(1)}) fusion(bf16[2048,512]{1,0:T(8,128)(2,1)S(1)} %copy-done, bf16[288,512]{1,0:T(8,128)(2,1)S(1)} %bitcast.48, bf16[512,2048]{1,0:T(8,128)(2,1)} %param.11), kind=kOutput, calls=%fused_computation.59 | convolution fusion | flops 1213415168 | bytes 5080192 | tf_op jit(solution)/shard_map/dot_general | solution.py:113
  74.8 0.2 multiply_reduce_fusion.2
  75.1 0.2 add_convert_fusion
  75.3 1.9 %collective-permute-start.4 = (bf16[2,6,6,512]{3,2,1,0:T(8,128)(2,1)S(1)}, bf16[2,6,6,512]{3,2,1,0:T(8,128)(2,1)S(1)}, u32[]{:S(2)}, u32[]{:S(2)}) collective-permute-start(bf16[2,6,6,512]{3,2,1,0:T(8,128)(2,1)S(1)} %slice.68), channel_id=1, source_target_pairs={{0,1},{1,2},{2,3},{3,4},{4,5},{5,6},{6,7},{7,8},{8,9},{9,10},{10,1... | collective-permute-start | bytes 221192 | tf_op jit(solution)/shard_map/ppermute | solution.py:22
  77.3 10.5 %collective-permute-done.4 = bf16[2,6,6,512]{3,2,1,0:T(8,128)(2,1)S(1)} collective-permute-done((bf16[2,6,6,512]{3,2,1,0:T(8,128)(2,1)S(1)}, bf16[2,6,6,512]{3,2,1,0:T(8,128)(2,1)S(1)}, u32[]{:S(2)}, u32[]{:S(2)}) %collective-permute-start.4) | collective-permute-done | bytes 73760 | tf_op jit(solution)/shard_map/ppermute | solution.py:22
  87.7 0.1 fusion.17
  87.8 7.9 %collective-permute-start.5 = (bf16[2,3,24,512]{3,2,1,0:T(8,128)(2,1)S(1)}, bf16[2,3,24,512]{3,2,1,0:T(8,128)(2,1)S(1)}, u32[]{:S(2)}, u32[]{:S(2)}) collective-permute-start(bf16[2,3,24,512]{3,2,1,0:T(8,128)(2,1)S(1)} %fusion.17), channel_id=1, source_target_pairs={{0,16},{16,32},{32,48},{48,64},{64,80},{80,96},{96,112},{112,128},... | collective-permute-start | bytes 442376 | tf_op jit(solution)/shard_map/ppermute | solution.py:22
  95.7 16.5 %collective-permute-done.5 = bf16[2,3,24,512]{3,2,1,0:T(8,128)(2,1)S(1)} collective-permute-done((bf16[2,3,24,512]{3,2,1,0:T(8,128)(2,1)S(1)}, bf16[2,3,24,512]{3,2,1,0:T(8,128)(2,1)S(1)}, u32[]{:S(2)}, u32[]{:S(2)}) %collective-permute-start.5) | collective-permute-done | bytes 147488 | tf_op jit(solution)/shard_map/ppermute | solution.py:22
  112.2 0.8 fusion.16
  (22 shorter events, 0.2 us)
Async XLA Ops:
  0.0 71.5 %copy-start = (bf16[2048,512]{1,0:T(8,128)(2,1)S(1)}, bf16[2048,512]{1,0:T(8,128)(2,1)}, u32[]{:S(2)}) copy-start(bf16[2048,512]{1,0:T(8,128)(2,1)} %param.12) | copy-start | bytes 6291460
  1.2 17.0 %collective-permute-start = (bf16[1,6,24,512]{3,2,1,0:T(8,128)(2,1)S(1)}, bf16[1,6,24,512]{3,2,1,0:T(8,128)(2,1)S(1)}, u32[]{:S(2)}, u32[]{:S(2)}) collective-permute-start(bf16[1,6,24,512]{3,2,1,0:T(8,128)(2,1)S(1)} %slice_select_fusion), channel_id=1, source_target_pairs={{0,512},{512,0},{1,513},{513,1},{2,514},{514,2},{3,515},{515,3},{4... | collective-permute-start | bytes 442376 | tf_op jit(solution)/shard_map/ppermute | solution.py:17
  19.3 15.4 %collective-permute-start.2 = (bf16[3,6,6,512]{3,2,1,0:T(8,128)(2,1)S(1)}, bf16[3,6,6,512]{3,2,1,0:T(8,128)(2,1)S(1)}, u32[]{:S(2)}, u32[]{:S(2)}) collective-permute-start(bf16[3,6,6,512]{3,2,1,0:T(8,128)(2,1)S(1)} %slice.62), channel_id=1, source_target_pairs={{0,15},{1,0},{2,1},{3,2},{4,3},{5,4},{6,5},{7,6},{8,7},{9,8},{10,9... | collective-permute-start | bytes 331784 | tf_op jit(solution)/shard_map/ppermute | solution.py:22
  21.3 28.4 %collective-permute-start.1 = (bf16[3,3,24,512]{3,2,1,0:T(8,128)(2,1)S(1)}, bf16[3,3,24,512]{3,2,1,0:T(8,128)(2,1)S(1)}, u32[]{:S(2)}, u32[]{:S(2)}) collective-permute-start(bf16[3,3,24,512]{3,2,1,0:T(8,128)(2,1)S(1)} %get-tuple-element.9), channel_id=1, source_target_pairs={{0,496},{16,0},{32,16},{48,32},{64,48},{80,64},{96,80},{112,96},{1... | collective-permute-start | bytes 663560 | tf_op jit(solution)/shard_map/ppermute | solution.py:22
  34.7 15.0 %collective-permute-start.3 = (bf16[3,3,6,512]{3,2,1,0:T(8,128)(2,1)S(1)}, bf16[3,3,6,512]{3,2,1,0:T(8,128)(2,1)S(1)}, u32[]{:S(2)}, u32[]{:S(2)}) collective-permute-start(bf16[3,3,6,512]{3,2,1,0:T(8,128)(2,1)S(1)} %get-tuple-element.11), channel_id=1, source_target_pairs={{0,496},{16,0},{32,16},{48,32},{64,48},{80,64},{96,80},{112,96},{1... | collective-permute-start | bytes 165896 | tf_op jit(solution)/shard_map/ppermute | solution.py:22
  49.9 0.8 copy-start.1
  59.0 4.1 %copy-start.6 = (f32[8]{0:T(128)S(1)}, f32[8]{0:T(128)}, u32[]{:S(2)}) copy-start(f32[8]{0:T(128)} %param.13) | copy-start | bytes 100
  63.1 1.5 %copy-start.3 = (bf16[2,216,512]{1,2,0:T(8,128)(2,1)S(1)}, bf16[2,216,512]{1,2,0:T(8,128)(2,1)}, u32[]{:S(2)}) copy-start(bf16[2,216,512]{1,2,0:T(8,128)(2,1)} %copy.11) | copy-start | bytes 1327108
  69.0 2.2 %copy-start.4 = (f32[512]{0:T(512)S(1)}, f32[512]{0:T(512)}, u32[]{:S(2)}) copy-start(f32[512]{0:T(512)} %param.14) | copy-start | bytes 6148
  69.2 2.0 %copy-start.2 = (bf16[3,6,24,512]{3,2,1,0:T(8,128)(2,1)S(1)}, bf16[3,6,24,512]{3,2,1,0:T(8,128)(2,1)}, u32[]{:S(2)}) copy-start(bf16[3,6,24,512]{3,2,1,0:T(8,128)(2,1)} %copy-done.1) | copy-start | bytes 1327108
  71.5 3.6 %copy-start.5 = (f32[512]{0:T(512)S(1)}, f32[512]{0:T(512)}, u32[]{:S(2)}) copy-start(f32[512]{0:T(512)} %param.15) | copy-start | bytes 6148
  75.3 12.4 %collective-permute-start.4 = (bf16[2,6,6,512]{3,2,1,0:T(8,128)(2,1)S(1)}, bf16[2,6,6,512]{3,2,1,0:T(8,128)(2,1)S(1)}, u32[]{:S(2)}, u32[]{:S(2)}) collective-permute-start(bf16[2,6,6,512]{3,2,1,0:T(8,128)(2,1)S(1)} %slice.68), channel_id=1, source_target_pairs={{0,1},{1,2},{2,3},{3,4},{4,5},{5,6},{6,7},{7,8},{8,9},{9,10},{10,1... | collective-permute-start | bytes 221192 | tf_op jit(solution)/shard_map/ppermute | solution.py:22
  87.8 24.4 %collective-permute-start.5 = (bf16[2,3,24,512]{3,2,1,0:T(8,128)(2,1)S(1)}, bf16[2,3,24,512]{3,2,1,0:T(8,128)(2,1)S(1)}, u32[]{:S(2)}, u32[]{:S(2)}) collective-permute-start(bf16[2,3,24,512]{3,2,1,0:T(8,128)(2,1)S(1)} %fusion.17), channel_id=1, source_target_pairs={{0,16},{16,32},{32,48},{48,64},{64,80},{80,96},{96,112},{112,128},... | collective-permute-start | bytes 442376 | tf_op jit(solution)/shard_map/ppermute | solution.py:22
where the time goes:
time: 113 us
  starting transfers between devices  44.5 us (39%)
  waiting for transfers between devices  39.2 us (35%)
  local copies, waits for them, and re-layouts  13.5 us (12%)
  matrix products  10.8 us (10%)
  other arithmetic  4.66 us (4%)
    ppermute x5, waiting for transfers between devices, from_behind(): lax.ppermute(array, axis, [(i, (i + by) % length) for i in range(length)])  38.5 us
    ppermute x5, starting transfers between devices, from_behind(): lax.ppermute(array, axis, [(i, (i + by) % length) for i in range(length)])  28.5 us
    ppermute x1, starting transfers between devices, from_partner(): return lax.ppermute(block, axis, route)  16 us
    dot_general x1, matrix products, per_device(): down = jnp.dot(hidden, w_down, preferred_element_type=jnp.float32)  3.36 us
    transpose x3, local copies, waits for them, and re-layouts, to_windows(): shaped = jnp.transpose(shaped, (0, 2, 4, 1, 3, 5, 6))  3.01 us
    slice x2, local copies, waits for them, and re-layouts, attend(): keys = packed[..., width:2 * width].reshape(count, span, heads, size)  2.32 us
    dot_general x1, matrix products, per_device(): jnp.dot(moved.reshape(-1, width), w_qkv, preferred_element_type=jnp.float32)  2.26 us
  transfers between devices with their start and end apart: 6, of which 4 were waited for; matrix products, arithmetic and copies ran while one was open for 0% of the time, Pallas kernels for 0%

commit v1 on v0

v1 whole, which is shorter than its diff:
```python
import functools
import math

import jax
import jax.numpy as jnp
import numpy as np
from jax import lax
from jax.experimental import pallas as pl
from jax.experimental.pallas import tpu as pltpu
from jax.sharding import PartitionSpec as P

WA = 6
WO = 12
LOG2E = 1.4426950408889634


def shift(array, axis, by):
    length = lax.axis_size(axis)
    return lax.ppermute(array, axis, [(i, (i + by) % length) for i in range(length)])


def swap(array, axis):
    length = lax.axis_size(axis)
    return lax.ppermute(array, axis, [(i, i ^ 1) for i in range(length)])


def edge_select(rows, cols):
    half = rows // 2
    edge = WO // 2
    own = rows * cols
    starts = (0, own, half * cols, own + half * cols)
    pick = np.zeros((2, 4, half, edge, 2 * own), np.float32)
    for side in range(2):
        for part in range(4):
            for row in range(half):
                for col in range(edge):
                    source = starts[part] + row * cols + col + side * (cols - edge)
                    pick[side, part, row, col, source] = 1
    return pick.reshape(2 * 4 * half * edge, 2 * own)


def key_table(rows, cols):
    half = rows // 2
    edge = WO // 2
    table = []
    for r in range(rows):
        for c in range(cols):
            table.append((r // half, (c + edge) // WO, 0))
    for h in range(2):
        for r in range(half):
            for c in range(cols):
                table.append((h, (c + edge) // WO, 1))
    for side in range(2):
        for part in range(4):
            for _ in range(half * edge):
                table.append((part // 2, side * (cols // WO), part % 2))
    return np.array(table, np.int32)


def edges_kernel(pick_ref, own_ref, above_ref, below_ref, left_ref, right_ref):
    levels = own_ref.shape[0]
    count = left_ref.shape[1]
    for level in range(levels):
        source = jnp.concatenate([own_ref[level], above_ref[level], below_ref[level]], 0)
        edges = jnp.dot(pick_ref[...], source, preferred_element_type=jnp.float32)
        edges = edges.astype(jnp.bfloat16)
        left_ref[level] = edges[:count]
        right_ref[level] = edges[count:]


def join_kernel(lev_ref, own_ref, above_ref, below_ref, left_ref, right_ref, alone_ref, paired_ref):
    lev = lev_ref[0]
    for level, out_ref in ((lev, alone_ref), (1 - lev, paired_ref)):
        at = 0
        for ref in (own_ref, above_ref, below_ref, left_ref, right_ref):
            count = ref.shape[1]
            out_ref[at : at + count, :] = ref[level]
            at += count


def layer_norm(values, gain):
    mean = jnp.mean(values, axis=-1, keepdims=True)
    centred = values - mean
    spread = jnp.mean(centred * centred, axis=-1, keepdims=True)
    return centred * lax.rsqrt(spread + 1e-05) * gain


def square_sums(values, heads_of):
    squares = values.astype(jnp.float32)
    squares = squares * squares
    high = squares.astype(jnp.bfloat16)
    low = (squares - high.astype(jnp.float32)).astype(jnp.bfloat16)
    return high, low


def contract_last(a, b):
    return lax.dot_general(a, b, (((1,), (1,)), ((), ())), preferred_element_type=jnp.float32)


def attend(query, keys, values, mask, logit, heads_of):
    count, width = query.shape
    heads = heads_of.shape[0]
    size = width // heads
    pair = 2 * size
    high, low = square_sums(query, heads_of)
    q_scale = contract_last(high, heads_of) + contract_last(low, heads_of)
    q_scale = lax.rsqrt(q_scale + 1e-06) * logit
    high, low = square_sums(keys, heads_of)
    k_scale = contract_last(heads_of, high) + contract_last(heads_of, low)
    k_scale = lax.rsqrt(k_scale + 1e-06)
    lane = lax.broadcasted_iota(jnp.int32, (count, pair), 1)
    ones = jnp.ones((keys.shape[0], pair), jnp.bfloat16)
    parts = []
    for p in range(heads // 2):
        q = query[:, p * pair : (p + 1) * pair]
        k = keys[:, p * pair : (p + 1) * pair]
        v = jnp.concatenate([values[:, p * pair : (p + 1) * pair], ones], 1)
        outs = []
        for side in range(2):
            h = 2 * p + side
            inside = (lane >= size) if side else (lane < size)
            raw = contract_last(jnp.where(inside, q, jnp.zeros_like(q)), k)
            scores = raw * q_scale[:, h : h + 1] * k_scale[h : h + 1, :]
            expd = (jnp.exp2(scores) * mask).astype(jnp.bfloat16)
            mixed = jnp.dot(expd, v, preferred_element_type=jnp.float32)
            outs.append(mixed[:, :pair] / mixed[:, pair:])
        parts.append(jnp.where(lane < size, outs[0], outs[1]).astype(jnp.bfloat16))
    return jnp.concatenate(parts, 1)


def block_kernel(
    lev_ref, alone_ref, paired_ref, other_ref, mask_ref, heads_ref, logit_ref,
    qkv_ref, proj_ref, up_ref, down_ref, gain_attn_ref, gain_mlp_ref,
    out_ref, kv_ref, mixed_ref,
):
    lev = lev_ref[0]
    width = proj_ref.shape[0]
    span = alone_ref.shape[0]
    own = mask_ref.shape[0]
    for i, ref in enumerate((alone_ref, paired_ref, other_ref)):
        kv = jnp.dot(ref[...], qkv_ref[:, width:], preferred_element_type=jnp.float32)
        kv_ref[i * span : (i + 1) * span, :] = kv.astype(jnp.bfloat16)
    mask = mask_ref[...]
    logit = logit_ref[...] * LOG2E
    heads_of = heads_ref[...]
    for i, (ref, first, last) in enumerate(((alone_ref, 0, span), (paired_ref, span, 3 * span))):
        query = jnp.dot(ref[:own, :], qkv_ref[:, :width], preferred_element_type=jnp.float32)
        keys = kv_ref[first:last, :width]
        values = kv_ref[first:last, width:]
        wide = mask if i == 0 else jnp.concatenate([mask, mask], 1)
        mixed_ref[i * own : (i + 1) * own, :] = attend(
            query.astype(jnp.bfloat16), keys, values, wide, logit, heads_of
        )
    attn_out = jnp.dot(mixed_ref[...], proj_ref[...], preferred_element_type=jnp.float32)
    attn_out = attn_out.astype(jnp.bfloat16).astype(jnp.float32)
    stream = jnp.concatenate([alone_ref[:own, :], paired_ref[:own, :]], 0).astype(jnp.float32)
    settled = (stream + layer_norm(attn_out, gain_attn_ref[...])).astype(jnp.bfloat16)
    hidden = jnp.dot(settled, up_ref[...], preferred_element_type=jnp.float32)
    hidden = jax.nn.gelu(hidden, approximate=True).astype(jnp.bfloat16)
    down = jnp.dot(hidden, down_ref[...], preferred_element_type=jnp.float32)
    result = settled.astype(jnp.float32) + layer_norm(down, gain_mlp_ref[...])
    result = result.astype(jnp.bfloat16)
    out_ref[lev] = result[:own]
    out_ref[1 - lev] = result[own:]


def in_vmem(count):
    return [pl.BlockSpec(memory_space=pltpu.VMEM)] * count


SCALAR = pl.BlockSpec(memory_space=pltpu.SMEM)


def per_device(grid, w_qkv, w_proj, w_up, w_down, logit_scale, gain_attn, gain_mlp):
    levels, rows, cols, width = grid.shape
    half = rows // 2
    edge = WO // 2
    own = rows * cols
    heads = logit_scale.shape[0]
    bf16 = jnp.bfloat16
    lev = lax.axis_index("lev").astype(jnp.int32).reshape(1)
    lat = lax.axis_index("lat")
    last = lax.axis_size("lat") - 1

    table = key_table(rows, cols)
    same = (table[:own, None, :2] == table[None, :, :2]).all(-1)
    upper = ((table[:, 0] == 0) & (table[:, 2] == 1)).astype(np.float32)
    lower = ((table[:, 0] == 1) & (table[:, 2] == 1)).astype(np.float32)
    open_keys = 1 - upper * (lat == 0) - lower * (lat == last)
    mask = jnp.asarray(same.astype(np.float32)) * open_keys[None, :]
    heads_of = np.repeat(np.eye(heads, dtype=np.float32), width // heads, axis=1)

    tokens = grid.reshape(levels, own, width)
    below = shift(tokens[:, : half * cols], "lat", -1)
    above = shift(tokens[:, half * cols :], "lat", 1)

    side = jax.ShapeDtypeStruct((levels, 4 * half * edge, width), bf16)
    left, right = pl.pallas_call(
        edges_kernel, out_shape=(side, side), in_specs=in_vmem(4), out_specs=tuple(in_vmem(2)),
        name="edges",
    )(jnp.asarray(edge_select(rows, cols), bf16), tokens, above, below)
    from_east = shift(left, "lon", -1)
    from_west = shift(right, "lon", 1)

    span = table.shape[0]
    flat = jax.ShapeDtypeStruct((span, width), bf16)
    alone, paired = pl.pallas_call(
        join_kernel, out_shape=(flat, flat), in_specs=[SCALAR] + in_vmem(5),
        out_specs=tuple(in_vmem(2)), name="join",
    )(lev, tokens, above, below, from_west, from_east)
    other = swap(paired, "lev")

    out = pl.pallas_call(
        block_kernel,
        out_shape=jax.ShapeDtypeStruct((levels, own, width), bf16),
        in_specs=[SCALAR] + in_vmem(12),
        out_specs=in_vmem(1)[0],
        scratch_shapes=[
            pltpu.VMEM((3 * span, 2 * width), bf16),
            pltpu.VMEM((levels * own, width), bf16),
        ],
        compiler_params=pltpu.CompilerParams(vmem_limit_bytes=48 << 20),
        name="block",
    )(
        lev, alone, paired, other, mask, jnp.asarray(heads_of, bf16), logit_scale.reshape(1, heads),
        w_qkv, w_proj, w_up, w_down, gain_attn.reshape(1, width), gain_mlp.reshape(1, width),
    )
    return out.reshape(levels, rows, cols, width)


def solution(mesh):
    placed = (P("lev", "lat", "lon", None), P(), P(), P(), P(), P(), P(), P())
    return jax.shard_map(
        per_device,
        mesh=mesh,
        in_specs=placed,
        out_specs=P("lev", "lat", "lon", None),
        check_vma=False,
    )
```

time: 113 us -> 82.2 us (0.73)
  waiting for transfers between devices: 39.2 us -> 13.5 us
  Pallas kernels: 0 us -> 14.2 us
  matrix products: 10.8 us -> 0 us
  local copies, waits for them, and re-layouts: 13.5 us -> 5.93 us
  other arithmetic: 4.66 us -> 1 us
  starting transfers between devices: 44.5 us -> 46.9 us
    ppermute x6 -> x5, waiting for transfers between devices: 39.2 us -> 13.5 us  [the longest x4 12.9 us: shift(): lax.ppermute(array, axis, [(i, (i + by) % length) for i in range(length)])]
    pallas_call x0 -> x3, Pallas kernels: none -> 14.2 us  [the longest x1 9.85 us: per_device(): pl.pallas_call(block_kernel, out_shape=jax.ShapeDtypeStruct((levels, own,...]
    dot_general x5 -> x0, matrix products: 10.8 us -> none  [the longest x1 3.36 us: per_device(): down = jnp.dot(hidden, w_down, preferred_element_type=jnp.float32)]
    slice x8 -> x1, local copies, waits for them, and re-layouts: 5.65 us -> 1.16 us  [per_device(): below = shift(tokens[:, :half * cols], 'lat', -1)]
    unnamed x14 -> x30, local copies, waits for them, and re-layouts: 0.8 us -> 4.78 us
    transpose x4 -> x0, local copies, waits for them, and re-layouts: 3.09 us -> none  [the longest x3 3.01 us: to_windows(): shaped = jnp.transpose(shaped, (0, 2, 4, 1, 3, 5, 6))]
    ppermute x6 -> x5, starting transfers between devices: 44.5 us -> 46.9 us  [the longest x4 42.5 us: shift(): lax.ppermute(array, axis, [(i, (i + by) % length) for i in range(length)])]
    select_n x2 -> x0, other arithmetic: 2.27 us -> none  [the longest x1 1.15 us: per_device(): inner = jnp.where(lev_index == 0, grid[1:2], grid[0:1])]
  transfers between devices with their start and end apart: 6 -> 5, of which waited for: 4 -> 5; matrix products, arithmetic and copies ran while one was open for 0% -> 1% of each run, Pallas kernels for 0% -> 0%
where the time goes in v1:
time: 82.2 us; the launch traced here: 81.7 us
  starting transfers between devices  46.9 us (57%)
  Pallas kernels  14.2 us (17%)
  waiting for transfers between devices  13.5 us (16%)
  local copies, waits for them, and re-layouts  5.93 us (7%)
  other arithmetic  1 us (1%)
    ppermute x4, starting transfers between devices, shift(): lax.ppermute(array, axis, [(i, (i + by) % length) for i in range(length)])  42.5 us
    ppermute x4, waiting for transfers between devices, shift(): lax.ppermute(array, axis, [(i, (i + by) % length) for i in range(length)])  12.9 us
    pallas_call x1, Pallas kernels, per_device(): pl.pallas_call(block_kernel, out_shape=jax.ShapeDtypeStruct((levels, own,...  9.85 us
    unnamed x30, local copies, waits for them, and re-layouts  4.78 us
    ppermute x1, starting transfers between devices, swap(): return lax.ppermute(array, axis, [(i, i ^ 1) for i in range(length)])  4.41 us
    pallas_call x1, Pallas kernels, per_device(): pl.pallas_call(join_kernel, out_shape=(flat, flat), in_specs=[SCALAR] + i...  2.17 us
    pallas_call x1, Pallas kernels, per_device(): pl.pallas_call(edges_kernel, out_shape=(side, side), in_specs=in_vmem(4),...  2.15 us
  transfers between devices with their start and end apart: 5, of which 5 were waited for; matrix products, arithmetic and copies ran while one was open for 1% of the time, Pallas kernels for 0%

profile of v1, /device:TPU:1, one launch (start us, length us, event | category | flops | bytes accessed | tf_op | source)
XLA Modules:
  0.0 81.7 jit_solution(10166636549350087734)
XLA Ops:
  0.0 0.0 copy-start.13
  0.0 0.0 copy-start.14
  0.0 0.0 copy-start.5
  0.0 0.0 copy-start.7
  0.0 0.0 copy-start.6
  0.0 0.0 copy-start.8
  0.0 0.0 copy-start
  0.0 0.0 copy-start.2
  0.1 1.2 %fusion = (bf16[2,72,512]{2,1,0:T(8,128)(2,1)S(1)}, bf16[2,72,512]{2,1,0:T(8,128)(2,1)S(1)}) fusion(bf16[2,144,512]{2,1,0:T(8,128)(2,1)} %bitcast.9), kind=kLoop, calls=%fused_computation.2 | loop fusion | bytes 589824 | tf_op jit(solution)/shard_map/slice | solution.py:194
  1.2 21.6 %collective-permute-start.1 = (bf16[2,72,512]{2,1,0:T(8,128)(2,1)S(1)}, bf16[2,72,512]{2,1,0:T(8,128)(2,1)S(1)}, u32[]{:S(2)}, u32[]{:S(2)}) collective-permute-start(bf16[2,72,512]{2,1,0:T(8,128)(2,1)S(1)} %get-tuple-element.13), channel_id=1, source_target_pairs={{0,496},{16,0},{32,16},{48,32},{64,48},{80,64},{96,80},{112,96},{1... | collective-permute-start | bytes 442376 | tf_op jit(solution)/shard_map/ppermute | solution.py:19
  22.9 1.9 %collective-permute-start = (bf16[2,72,512]{2,1,0:T(8,128)(2,1)S(1)}, bf16[2,72,512]{2,1,0:T(8,128)(2,1)S(1)}, u32[]{:S(2)}, u32[]{:S(2)}) collective-permute-start(bf16[2,72,512]{2,1,0:T(8,128)(2,1)S(1)} %get-tuple-element.14), channel_id=1, source_target_pairs={{0,16},{16,32},{32,48},{48,64},{64,80},{80,96},{96,112},{112,128},... | collective-permute-start | bytes 442376 | tf_op jit(solution)/shard_map/ppermute | solution.py:19
  24.8 1.7 %collective-permute-done.1.below_ref = bf16[2,72,512]{2,1,0:T(8,128)(2,1)S(1)} collective-permute-done((bf16[2,72,512]{2,1,0:T(8,128)(2,1)S(1)}, bf16[2,72,512]{2,1,0:T(8,128)(2,1)S(1)}, u32[]{:S(2)}, u32[]{:S(2)}) %collective-permute-start.1) | collective-permute-done | bytes 147488 | tf_op jit(solution)/shard_map/ppermute | solution.py:19
  26.5 0.0 copy-start.9
  26.5 8.8 %collective-permute-done.above_ref = bf16[2,72,512]{2,1,0:T(8,128)(2,1)S(1)} collective-permute-done((bf16[2,72,512]{2,1,0:T(8,128)(2,1)S(1)}, bf16[2,72,512]{2,1,0:T(8,128)(2,1)S(1)}, u32[]{:S(2)}, u32[]{:S(2)}) %collective-permute-start) | collective-permute-done | bytes 147488 | tf_op jit(solution)/shard_map/ppermute | solution.py:19
  35.3 0.0 copy-done.9
  35.3 0.0 copy-start.10
  35.3 0.7 copy-done.10
  36.0 2.1 %edges.1 = (bf16[2,72,512]{2,1,0:T(8,128)(2,1)}, bf16[2,72,512]{2,1,0:T(8,128)(2,1)}) custom-call(bf16[144,288]{1,0:T(8,128)(2,1)} %constant.31.clone.pick_ref, bf16[2,144,512]{2,1,0:T(8,128)(2,1)} %bitcast.10, bf16[2,72,512]{2,1,0:T(8,128)(2,1)} %copy-done.10, bf16[2,72,512]{2,1,0:T(8,128)(2,1)} %copy-done.9), custom_call_target="tpu_custom_call" | custom-call | tf_op jit(solution)/shard_map/edges/pallas_call | solution.py:198
  38.1 3.3 %collective-permute-start.2 = (bf16[2,72,512]{2,1,0:T(8,128)(2,1)}, bf16[2,72,512]{2,1,0:T(8,128)(2,1)S(1)}, u32[]{:S(2)}, u32[]{:S(2)}) collective-permute-start(bf16[2,72,512]{2,1,0:T(8,128)(2,1)} %get-tuple-element.9), channel_id=1, source_target_pairs={{0,1},{1,2},{2,3},{3,4},{4,5},{5,6},{6,7},{7,8},{8,9},{9,10},{10,1... | collective-permute-start | bytes 442376 | tf_op jit(solution)/shard_map/ppermute | solution.py:19
  41.4 15.7 %collective-permute-start.3 = (bf16[2,72,512]{2,1,0:T(8,128)(2,1)}, bf16[2,72,512]{2,1,0:T(8,128)(2,1)S(1)}, u32[]{:S(2)}, u32[]{:S(2)}) collective-permute-start(bf16[2,72,512]{2,1,0:T(8,128)(2,1)} %get-tuple-element.10), channel_id=1, source_target_pairs={{0,15},{1,0},{2,1},{3,2},{4,3},{5,4},{6,5},{7,6},{8,7},{9,8},{10,9... | collective-permute-start | bytes 442376 | tf_op jit(solution)/shard_map/ppermute | solution.py:19
  57.1 0.8 collective-permute-done.2.left_ref
  57.9 0.0 copy-start.11
  57.9 1.6 %collective-permute-done.3.right_ref = bf16[2,72,512]{2,1,0:T(8,128)(2,1)S(1)} collective-permute-done((bf16[2,72,512]{2,1,0:T(8,128)(2,1)}, bf16[2,72,512]{2,1,0:T(8,128)(2,1)S(1)}, u32[]{:S(2)}, u32[]{:S(2)}) %collective-permute-start.3) | collective-permute-done | bytes 147488 | tf_op jit(solution)/shard_map/ppermute | solution.py:19
  59.5 0.0 copy-start.12
  59.5 0.0 copy-done.11
  59.5 0.6 copy-done.12
  60.1 2.2 %join.1 = (bf16[432,512]{1,0:T(8,128)(2,1)}, bf16[432,512]{1,0:T(8,128)(2,1)}) custom-call(s32[1]{0:T(128)} %bitcast.lev_ref, bf16[2,144,512]{2,1,0:T(8,128)(2,1)} %bitcast.11, bf16[2,72,512]{2,1,0:T(8,128)(2,1)} %copy-done.10, bf16[2,72,512]{2,1,0:T(8,128)(2,1)} %copy-done.9, bf16[2,72,512]{2,1,0:T(8,128)(2,1)} %copy-done.11, bf16[2,72,512]{2,1,0:T(8,128)(2,1)} %copy-done.12), custom_call_target="tpu_custom_call" | custom-call | tf_op jit(solution)/shard_map/join/pallas_call | solution.py:207
  62.3 4.4 %collective-permute-start.4 = (bf16[432,512]{1,0:T(8,128)(2,1)}, bf16[432,512]{1,0:T(8,128)(2,1)S(1)}, u32[]{:S(2)}, u32[]{:S(2)}) collective-permute-start(bf16[432,512]{1,0:T(8,128)(2,1)} %get-tuple-element.12.paired_ref), channel_id=1, source_target_pairs={{0,512},{512,0},{1,513},{513,1},{2,514},{514,2},{3,515},{515,3},{4... | collective-permute-start | bytes 1327112 | tf_op jit(solution)/shard_map/ppermute | solution.py:24
  66.7 0.0 copy-done.13
  66.7 0.0 copy-done.14
  66.8 1.0 %broadcast_multiply_fusion.mask_ref = f32[144,432]{1,0:T(8,128)S(1)} fusion(f32[144,432]{1,0:T(8,128)} %constant.30.clone, f32[432]{0:T(512)S(1)} %multiply_subtract_fusion), kind=kLoop, calls=%fused_computation | loop fusion | flops 62208 | bytes 499392 | tf_op jit(solution)/shard_map/mul | solution.py:190
  67.8 0.6 collective-permute-done.4.other_ref
  68.3 0.0 copy-done.5
  68.3 0.0 copy-done.7
  68.3 0.0 copy-done.6
  68.3 0.0 copy-done.8
  68.3 0.0 copy-done
  68.4 0.0 copy-done.2
  68.4 0.0 copy-start.1
  68.4 1.4 %copy-done.1 = bf16[512,1536]{1,0:T(8,128)(2,1)S(1)} copy-done((bf16[512,1536]{1,0:T(8,128)(2,1)S(1)}, bf16[512,1536]{1,0:T(8,128)(2,1)}, u32[]{:S(2)}) %copy-start.1) | copy-done | bytes 1572888
  69.8 0.0 copy-start.3
  69.8 1.0 %copy-done.3 = bf16[432,512]{1,0:T(8,128)(2,1)S(1)} copy-done((bf16[432,512]{1,0:T(8,128)(2,1)S(1)}, bf16[432,512]{1,0:T(8,128)(2,1)}, u32[]{:S(2)}) %copy-start.3) | copy-done | bytes 442392
  70.8 0.0 copy-start.4
  70.8 1.0 %copy-done.4 = bf16[432,512]{1,0:T(8,128)(2,1)S(1)} copy-done((bf16[432,512]{1,0:T(8,128)(2,1)S(1)}, bf16[432,512]{1,0:T(8,128)(2,1)}, u32[]{:S(2)}) %copy-start.4) | copy-done | bytes 442392
  71.8 9.9 %block.1 = bf16[2,144,512]{2,1,0:T(8,128)(2,1)} custom-call(s32[1]{0:T(128)} %bitcast.lev_ref, bf16[432,512]{1,0:T(8,128)(2,1)S(1)} %copy-done.3, bf16[432,512]{1,0:T(8,128)(2,1)S(1)} %copy-done.4, bf16[432,512]{1,0:T(8,128)(2,1)S(1)} %collective-permute-done.4.other_ref, f32[144,432]{1,0:T(8,128)S(1)} %broadcast_multiply_fusion.mask_ref, ...), custom_call_target="tpu_custom_call" | custom-call | tf_op jit(solution)/shard_map/block/pallas_call | solution.py:213
  (1 shorter events, 0.0 us)
Async XLA Ops:
  0.0 66.7 %copy-start.13 = (f32[432]{0:T(512)S(1)}, f32[432]{0:T(512)}, u32[]{:S(2)}) copy-start(f32[432]{0:T(512)} %constant.29.clone) | copy-start | bytes 5188
  0.0 66.7 %copy-start.14 = (f32[432]{0:T(512)S(1)}, f32[432]{0:T(512)}, u32[]{:S(2)}) copy-start(f32[432]{0:T(512)} %constant.28.clone) | copy-start | bytes 5188
  0.0 68.3 %copy-start.5 = (bf16[8,512]{1,0:T(8,128)(2,1)S(1)}, bf16[8,512]{1,0:T(8,128)(2,1)}, u32[]{:S(2)}) copy-start(bf16[8,512]{1,0:T(8,128)(2,1)} %constant.32.clone.heads_ref) | copy-start | bytes 24580
  0.0 68.3 %copy-start.7 = (f32[512]{0:T(512)S(1)}, f32[512]{0:T(512)}, u32[]{:S(2)}) copy-start(f32[512]{0:T(512)} %param.20) | copy-start | bytes 6148
  0.0 68.3 %copy-start.6 = (f32[512]{0:T(512)S(1)}, f32[512]{0:T(512)}, u32[]{:S(2)}) copy-start(f32[512]{0:T(512)} %param.19) | copy-start | bytes 6148
  0.0 68.3 %copy-start.8 = (f32[8]{0:T(128)S(1)}, f32[8]{0:T(128)}, u32[]{:S(2)}) copy-start(f32[8]{0:T(128)} %param.18) | copy-start | bytes 100
  0.0 68.3 %copy-start = (bf16[512,2048]{1,0:T(8,128)(2,1)S(1)}, bf16[512,2048]{1,0:T(8,128)(2,1)}, u32[]{:S(2)}) copy-start(bf16[512,2048]{1,0:T(8,128)(2,1)} %up_ref.1) | copy-start | bytes 6291460
  0.0 68.3 %copy-start.2 = (bf16[512,512]{1,0:T(8,128)(2,1)S(1)}, bf16[512,512]{1,0:T(8,128)(2,1)}, u32[]{:S(2)}) copy-start(bf16[512,512]{1,0:T(8,128)(2,1)} %proj_ref.1) | copy-start | bytes 1572868
  1.2 25.3 %collective-permute-start.1 = (bf16[2,72,512]{2,1,0:T(8,128)(2,1)S(1)}, bf16[2,72,512]{2,1,0:T(8,128)(2,1)S(1)}, u32[]{:S(2)}, u32[]{:S(2)}) collective-permute-start(bf16[2,72,512]{2,1,0:T(8,128)(2,1)S(1)} %get-tuple-element.13), channel_id=1, source_target_pairs={{0,496},{16,0},{32,16},{48,32},{64,48},{80,64},{96,80},{112,96},{1... | collective-permute-start | bytes 442376 | tf_op jit(solution)/shard_map/ppermute | solution.py:19
  22.9 12.4 %collective-permute-start = (bf16[2,72,512]{2,1,0:T(8,128)(2,1)S(1)}, bf16[2,72,512]{2,1,0:T(8,128)(2,1)S(1)}, u32[]{:S(2)}, u32[]{:S(2)}) collective-permute-start(bf16[2,72,512]{2,1,0:T(8,128)(2,1)S(1)} %get-tuple-element.14), channel_id=1, source_target_pairs={{0,16},{16,32},{32,48},{48,64},{64,80},{80,96},{96,112},{112,128},... | collective-permute-start | bytes 442376 | tf_op jit(solution)/shard_map/ppermute | solution.py:19
  26.5 8.8 %copy-start.9 = (bf16[2,72,512]{2,1,0:T(8,128)(2,1)}, bf16[2,72,512]{2,1,0:T(8,128)(2,1)S(1)}, u32[]{:S(2)}) copy-start(bf16[2,72,512]{2,1,0:T(8,128)(2,1)S(1)} %collective-permute-done.1.below_ref) | copy-start | bytes 442372
  35.3 0.7 copy-start.10
  38.1 19.8 %collective-permute-start.2 = (bf16[2,72,512]{2,1,0:T(8,128)(2,1)}, bf16[2,72,512]{2,1,0:T(8,128)(2,1)S(1)}, u32[]{:S(2)}, u32[]{:S(2)}) collective-permute-start(bf16[2,72,512]{2,1,0:T(8,128)(2,1)} %get-tuple-element.9), channel_id=1, source_target_pairs={{0,1},{1,2},{2,3},{3,4},{4,5},{5,6},{6,7},{7,8},{8,9},{9,10},{10,1... | collective-permute-start | bytes 442376 | tf_op jit(solution)/shard_map/ppermute | solution.py:19
  41.4 18.1 %collective-permute-start.3 = (bf16[2,72,512]{2,1,0:T(8,128)(2,1)}, bf16[2,72,512]{2,1,0:T(8,128)(2,1)S(1)}, u32[]{:S(2)}, u32[]{:S(2)}) collective-permute-start(bf16[2,72,512]{2,1,0:T(8,128)(2,1)} %get-tuple-element.10), channel_id=1, source_target_pairs={{0,15},{1,0},{2,1},{3,2},{4,3},{5,4},{6,5},{7,6},{8,7},{9,8},{10,9... | collective-permute-start | bytes 442376 | tf_op jit(solution)/shard_map/ppermute | solution.py:19
  57.9 1.6 %copy-start.11 = (bf16[2,72,512]{2,1,0:T(8,128)(2,1)}, bf16[2,72,512]{2,1,0:T(8,128)(2,1)S(1)}, u32[]{:S(2)}) copy-start(bf16[2,72,512]{2,1,0:T(8,128)(2,1)S(1)} %collective-permute-done.2.left_ref) | copy-start | bytes 442372
  59.5 0.7 copy-start.12
  62.3 6.0 %collective-permute-start.4 = (bf16[432,512]{1,0:T(8,128)(2,1)}, bf16[432,512]{1,0:T(8,128)(2,1)S(1)}, u32[]{:S(2)}, u32[]{:S(2)}) collective-permute-start(bf16[432,512]{1,0:T(8,128)(2,1)} %get-tuple-element.12.paired_ref), channel_id=1, source_target_pairs={{0,512},{512,0},{1,513},{513,1},{2,514},{514,2},{3,515},{515,3},{4... | collective-permute-start | bytes 1327112 | tf_op jit(solution)/shard_map/ppermute | solution.py:24
  68.4 1.4 %copy-start.1 = (bf16[512,1536]{1,0:T(8,128)(2,1)S(1)}, bf16[512,1536]{1,0:T(8,128)(2,1)}, u32[]{:S(2)}) copy-start(bf16[512,1536]{1,0:T(8,128)(2,1)} %qkv_ref.1) | copy-start | bytes 4718596
  69.8 1.0 %copy-start.3 = (bf16[432,512]{1,0:T(8,128)(2,1)S(1)}, bf16[432,512]{1,0:T(8,128)(2,1)}, u32[]{:S(2)}) copy-start(bf16[432,512]{1,0:T(8,128)(2,1)} %get-tuple-element.11.alone_ref) | copy-start | bytes 1327108
  70.8 1.0 %copy-start.4 = (bf16[432,512]{1,0:T(8,128)(2,1)S(1)}, bf16[432,512]{1,0:T(8,128)(2,1)}, u32[]{:S(2)}) copy-start(bf16[432,512]{1,0:T(8,128)(2,1)} %get-tuple-element.12.paired_ref) | copy-start | bytes 1327108

commit v2 on v0

v2 whole, which is shorter than its diff:
```python
import jax
import jax.numpy as jnp
import numpy as np
from jax import lax
from jax.experimental import pallas as pl
from jax.experimental.pallas import tpu as pltpu
from jax.sharding import PartitionSpec as P


WA = 6
WO = 12
EDGE = WO // 2
LOG2E = 1.4426950408889634
AXES = ("lev", "lat", "lon")


def send(array, target):
    sizes = [lax.axis_size(axis) for axis in AXES]
    route = []
    for lev in range(sizes[0]):
        for lat in range(sizes[1]):
            for lon in range(sizes[2]):
                at = [lev, lat, lon]
                to = [t % size for t, size in zip(target(lev, lat, lon), sizes)]
                flat = [(p[0] * sizes[1] + p[1]) * sizes[2] + p[2] for p in (at, to)]
                route.append(tuple(flat))
    return lax.ppermute(array, AXES, route)


def column_group(cols, first, last):
    own = [r * cols + c for r in range(WA) for c in range(first, last)]
    halo = [WA * cols + r * cols + c for r in range(WA) for c in range(first, last)]
    return own + halo


def one_hot(indices, size):
    table = np.zeros((len(indices), size), np.float32)
    for row, index in enumerate(indices):
        if index >= 0:
            table[row, index] = 1
    return jnp.asarray(table, jnp.bfloat16)


def gather_kernel(lev_ref, pick_ref, own_ref, first_ref, second_ref, alone_ref, paired_ref, west_ref, cross_ref):
    lev = lev_ref[0]
    kept = alone_ref.shape[0]
    edge = cross_ref.shape[0]
    for i, (level, out_ref) in enumerate(((lev, alone_ref), (1 - lev, paired_ref))):
        source = jnp.concatenate([own_ref[level], first_ref[level], second_ref[level]], 0)
        picked = jnp.dot(pick_ref[...], source, preferred_element_type=jnp.float32)
        picked = picked.astype(jnp.bfloat16)
        out_ref[...] = picked[:kept]
        west_ref[i * edge : (i + 1) * edge, :] = picked[kept:]
        if i == 1:
            cross_ref[...] = picked[kept:]


def load_kernel(*refs):
    count = len(refs) // 2
    sems = refs[-1]
    copies = [pltpu.make_async_copy(refs[i], refs[count + i], sems.at[i]) for i in range(count)]
    for copy in copies:
        copy.start()
    for copy in copies:
        copy.wait()


def load(*args):
    return pl.pallas_call(
        load_kernel,
        out_shape=tuple(jax.ShapeDtypeStruct(a.shape, a.dtype) for a in args),
        in_specs=[pl.BlockSpec(memory_space=pltpu.HBM)] * len(args),
        out_specs=(VMEM,) * len(args),
        scratch_shapes=[pltpu.SemaphoreType.DMA((len(args),))],
        compiler_params=pltpu.CompilerParams(vmem_limit_bytes=10 << 20),
        name="load",
    )(*(pltpu.with_memory_space_constraint(a, pltpu.HBM) for a in args))


def layer_norm(values, gain):
    mean = jnp.mean(values, axis=-1, keepdims=True)
    centred = values - mean
    spread = jnp.mean(centred * centred, axis=-1, keepdims=True)
    return centred * lax.rsqrt(spread + 1e-05) * gain


def split_squares(values):
    squares = values.astype(jnp.float32)
    squares = squares * squares
    high = squares.astype(jnp.bfloat16)
    low = (squares - high.astype(jnp.float32)).astype(jnp.bfloat16)
    return high, low


def contract_last(a, b):
    return lax.dot_general(a, b, (((1,), (1,)), ((), ())), preferred_element_type=jnp.float32)


def attend(query, keys, values, allowed, logit, heads_of):
    count, width = query.shape
    heads = heads_of.shape[0]
    size = width // heads
    pair = 2 * size
    high, low = split_squares(query)
    q_scale = contract_last(high, heads_of) + contract_last(low, heads_of)
    q_scale = lax.rsqrt(q_scale + 1e-06) * logit
    high, low = split_squares(keys)
    k_scale = contract_last(heads_of, high) + contract_last(heads_of, low)
    k_scale = lax.rsqrt(k_scale + 1e-06)
    lane = lax.broadcasted_iota(jnp.int32, (count, pair), 1)
    zero = jnp.zeros((count, pair), jnp.bfloat16)
    ones = jnp.ones((keys.shape[0], pair), jnp.bfloat16)
    parts = []
    for p in range(heads // 2):
        q = query[:, p * pair : (p + 1) * pair]
        k = keys[:, p * pair : (p + 1) * pair]
        v = jnp.concatenate([values[:, p * pair : (p + 1) * pair], ones], 1)
        both = jnp.concatenate([jnp.where(lane < size, q, zero), jnp.where(lane < size, zero, q)], 0)
        raw = contract_last(both, k)
        expd = []
        for side in range(2):
            h = 2 * p + side
            scores = raw[side * count : (side + 1) * count] * q_scale[:, h : h + 1] * k_scale[h : h + 1, :]
            expd.append((jnp.exp2(scores) * allowed).astype(jnp.bfloat16))
        mixed = jnp.dot(jnp.concatenate(expd, 0), v, preferred_element_type=jnp.float32)
        mixed = mixed[:, :pair] / mixed[:, pair:]
        parts.append(jnp.where(lane < size, mixed[:count], mixed[count:]).astype(jnp.bfloat16))
    return jnp.concatenate(parts, 1)


def allowed_keys(place_ref, queries, group, swapped):
    lev = place_ref[0]
    shape = (queries, 2 * queries)
    row = lax.broadcasted_iota(jnp.int32, shape, 0)
    col = lax.broadcasted_iota(jnp.int32, shape, 1)
    row = lax.rem(row, group)
    col = lax.rem(col, 2 * group)
    quarter = group // 2
    q_half = jnp.where(row < quarter, 0, 1)
    first = lev if swapped else 1 - lev
    k_half = jnp.where(col < quarter, 0, jnp.where(col < 2 * quarter, 1, jnp.where(col < 3 * quarter, first, 1 - first)))
    closed = jnp.where(k_half == 0, place_ref[1], place_ref[2])
    return jnp.where((q_half == k_half) & ((col < group) | (closed == 0)), 1.0, 0.0)


def run_windows(sources, query, place_ref, group, heads_ref, logit_ref, weights, kv_ref):
    qkv_ref, proj_ref, up_ref, down_ref, gain_attn_ref, gain_mlp_ref = weights
    width = proj_ref.shape[0]
    tokens = kv_ref.shape[0]
    span = tokens // 3
    count = span // 2
    kv = jnp.dot(sources, qkv_ref[:, width:], preferred_element_type=jnp.float32)
    kv_ref[...] = kv.astype(jnp.bfloat16)
    q = jnp.dot(query, qkv_ref[:, :width], preferred_element_type=jnp.float32).astype(jnp.bfloat16)
    own = allowed_keys(place_ref, count, group, False)
    other = allowed_keys(place_ref, count, group, True)
    logit = logit_ref[...] * LOG2E
    mixed = []
    for i, (first, last, allowed) in enumerate(((0, span, own), (span, tokens, jnp.concatenate([own, other], 1)))):
        keys = kv_ref[first:last, :width]
        values = kv_ref[first:last, width:]
        mixed.append(attend(q[i * count : (i + 1) * count], keys, values, allowed, logit, heads_ref[...]))
    mixed = jnp.concatenate(mixed, 0)
    attn_out = jnp.dot(mixed, proj_ref[...], preferred_element_type=jnp.float32)
    attn_out = attn_out.astype(jnp.bfloat16).astype(jnp.float32)
    settled = (query.astype(jnp.float32) + layer_norm(attn_out, gain_attn_ref[...])).astype(jnp.bfloat16)
    hidden = jnp.dot(settled, up_ref[...], preferred_element_type=jnp.float32)
    hidden = jax.nn.gelu(hidden, approximate=True).astype(jnp.bfloat16)
    down = jnp.dot(hidden, down_ref[...], preferred_element_type=jnp.float32)
    result = settled.astype(jnp.float32) + layer_norm(down, gain_mlp_ref[...])
    return result.astype(jnp.bfloat16)


def border_kernel(
    place_ref, alone_ref, paired_ref, other_ref, east_ref, cross_ref, pick_ref, back_ref, heads_ref, logit_ref,
    qkv_ref, proj_ref, up_ref, down_ref, gain_attn_ref, gain_mlp_ref, out_ref, return_ref, kv_ref,
):
    edge = cross_ref.shape[0]
    start = alone_ref.shape[0] - edge
    pieces = (
        alone_ref[start:, :], east_ref[:edge, :], paired_ref[start:, :], east_ref[edge:, :],
        other_ref[start:, :], cross_ref[...],
    )
    sources = jnp.concatenate(pieces, 0)
    query = [
        jnp.dot(pick_ref[...], sources[i * 2 * edge : (i + 1) * 2 * edge], preferred_element_type=jnp.float32)
        for i in range(2)
    ]
    query = jnp.concatenate(query, 0).astype(jnp.bfloat16)
    weights = (qkv_ref, proj_ref, up_ref, down_ref, gain_attn_ref, gain_mlp_ref)
    result = run_windows(sources, query, place_ref, edge // 2, heads_ref, logit_ref, weights, kv_ref)
    out_ref[...] = result
    back = jnp.dot(back_ref[...], result, preferred_element_type=jnp.float32)
    return_ref[...] = back.astype(jnp.bfloat16)


def middle_kernel(
    place_ref, alone_ref, paired_ref, other_ref, border_ref, middle_to_ref, border_to_ref, heads_ref, logit_ref,
    qkv_ref, proj_ref, up_ref, down_ref, gain_attn_ref, gain_mlp_ref, out_ref, kv_ref,
):
    lev = place_ref[0]
    span = kv_ref.shape[0] // 3
    count = span // 2
    sources = jnp.concatenate([alone_ref[:span, :], paired_ref[:span, :], other_ref[:span, :]], 0)
    query = jnp.concatenate([alone_ref[:count, :], paired_ref[:count, :]], 0)
    weights = (qkv_ref, proj_ref, up_ref, down_ref, gain_attn_ref, gain_mlp_ref)
    result = run_windows(sources, query, place_ref, count, heads_ref, logit_ref, weights, kv_ref)
    for i, level in enumerate((lev, 1 - lev)):
        placed = jnp.dot(middle_to_ref[...], result[i * count : (i + 1) * count], preferred_element_type=jnp.float32)
        placed += jnp.dot(border_to_ref[...], border_ref[i * count : (i + 1) * count, :], preferred_element_type=jnp.float32)
        out_ref[level] = placed.astype(jnp.bfloat16)


def place_kernel(place_ref, partial_ref, returned_ref, returned_to_ref, out_ref):
    lev = place_ref[0]
    own = partial_ref.shape[1]
    for i, level in enumerate((lev, 1 - lev)):
        placed = jnp.dot(
            returned_to_ref[i * own : (i + 1) * own, :], returned_ref[...], preferred_element_type=jnp.float32
        )
        row = lax.broadcasted_iota(jnp.int32, placed.shape, 0)
        mine = lax.rem(row, own // WA) >= EDGE
        out_ref[level] = jnp.where(mine, partial_ref[level], placed.astype(jnp.bfloat16))


VMEM = pl.BlockSpec(memory_space=pltpu.VMEM)
SMEM = pl.BlockSpec(memory_space=pltpu.SMEM)


def call(kernel, outs, megabytes, scratch=()):
    def run(place, *args):
        return pl.pallas_call(
            kernel,
            out_shape=outs,
            in_specs=[SMEM] + [VMEM] * len(args),
            out_specs=jax.tree.map(lambda _: VMEM, outs),
            scratch_shapes=list(scratch),
            compiler_params=pltpu.CompilerParams(vmem_limit_bytes=megabytes << 20),
        )(place, *args)

    return run


def per_device(grid, w_qkv, w_proj, w_up, w_down, logit_scale, gain_attn, gain_mlp):
    levels, rows, cols, width = grid.shape
    own = rows * cols
    half = own // 2
    edge = 2 * WA * EDGE
    heads = logit_scale.shape[0]
    bf16 = jnp.bfloat16

    def shape(*dims):
        return jax.ShapeDtypeStruct(dims, bf16)

    lev = lax.axis_index("lev").astype(jnp.int32)
    lat = lax.axis_index("lat")
    last = lax.axis_size("lat") - 1
    place = jnp.stack([lev, (lat == 0).astype(jnp.int32), (lat == last).astype(jnp.int32)])

    tokens = grid.reshape(levels, own, width)
    halves = grid.reshape(levels, 2, half, width)
    sent_first = lax.dynamic_index_in_dim(halves, lev, 1, keepdims=False)
    sent_second = lax.dynamic_index_in_dim(halves, 1 - lev, 1, keepdims=False)
    first = send(sent_first, lambda c, i, j: (c, i + 2 * c - 1, j))
    second = send(sent_second, lambda c, i, j: (c, i + 1 - 2 * c, j))

    groups = column_group(cols, EDGE, EDGE + WO) + column_group(cols, EDGE + WO, cols) + column_group(cols, 0, EDGE)
    heads_of = jnp.asarray(np.repeat(np.eye(heads, dtype=np.float32), width // heads, axis=1), bf16)
    quarter = edge // 2
    spots = [(r, c) for r in range(rows) for c in range(cols)]
    pick = [edge + t for t in range(quarter)] + list(range(quarter))
    back = [i * edge + t for i in range(2) for t in range(quarter)]
    middle_to = [r * WO + c - EDGE if EDGE <= c < EDGE + WO else -1 for r, c in spots]
    border_to = [quarter + r * EDGE + c - EDGE - WO if c >= EDGE + WO else -1 for r, c in spots]
    returned_to = [i * quarter + r * EDGE + c if c < EDGE else -1 for i in range(2) for r, c in spots]
    tokens, groups, pick, back, middle_to, border_to, returned_to, *shared = load(
        tokens, one_hot(groups, 2 * own), one_hot(pick, 2 * edge), one_hot(back, 2 * edge), one_hot(middle_to, edge),
        one_hot(border_to, edge), one_hot(returned_to, edge),
        heads_of, logit_scale.reshape(1, heads), w_qkv, w_proj, w_up, w_down,
        gain_attn.reshape(1, width), gain_mlp.reshape(1, width),
    )

    kept = 2 * own - edge
    outs = (shape(kept, width), shape(kept, width), shape(2 * edge, width), shape(edge, width))
    alone, paired, west, west_paired = call(gather_kernel, outs, 8)(place, groups, tokens, first, second)
    east = send(west, lambda c, i, j: (c, i, j - 1))
    cross = send(west_paired, lambda c, i, j: (1 - c, i, j - 1))
    other = send(paired, lambda c, i, j: (1 - c, i, j))

    kv = [pltpu.VMEM((6 * edge, 2 * width), bf16)]
    border, returning = call(border_kernel, (shape(2 * edge, width), shape(edge, width)), 16, kv)(
        place, alone, paired, other, east, cross, pick, back, *shared
    )
    returned = send(returning, lambda c, i, j: (c, i, j + 1))
    partial = call(middle_kernel, shape(levels, own, width), 16, kv)(
        place, alone, paired, other, border, middle_to, border_to, *shared
    )
    out = call(place_kernel, shape(levels, own, width), 8)(place, partial, returned, returned_to)
    return out.reshape(levels, rows, cols, width)


def solution(mesh):
    placed = (P("lev", "lat", "lon", None), P(), P(), P(), P(), P(), P(), P())
    return jax.shard_map(
        per_device,
        mesh=mesh,
        in_specs=placed,
        out_specs=P("lev", "lat", "lon", None),
        check_vma=False,
    )
```

time: 113 us -> 71.1 us (0.63)
  waiting for transfers between devices: 39.2 us -> 14.1 us
  Pallas kernels: 0 us -> 14.4 us
  local copies, waits for them, and re-layouts: 13.5 us -> 1 us
  matrix products: 10.8 us -> 0 us
  other arithmetic: 4.66 us -> 0.08 us
  starting transfers between devices: 44.5 us -> 41.1 us
    ppermute x6, waiting for transfers between devices: 39.2 us -> 14.1 us  [send(): return lax.ppermute(array, AXES, route)]
    pallas_call x0 -> x5, Pallas kernels: none -> 14.4 us  [the longest x4 11 us: run(): pl.pallas_call(kernel, out_shape=outs, in_specs=[SMEM] + [VMEM] * len(arg...]
    dot_general x5 -> x0, matrix products: 10.8 us -> none  [the longest x1 3.36 us: per_device(): down = jnp.dot(hidden, w_down, preferred_element_type=jnp.float32)]
    slice x8 -> x0, local copies, waits for them, and re-layouts: 5.65 us -> none  [the longest x2 2.32 us: attend(): keys = packed[..., width:2 * width].reshape(count, span, heads, size)]
    ppermute x6, starting transfers between devices: 44.5 us -> 41.1 us  [send(): return lax.ppermute(array, AXES, route)]
    transpose x4 -> x0, local copies, waits for them, and re-layouts: 3.09 us -> none  [the longest x3 3.01 us: to_windows(): shaped = jnp.transpose(shaped, (0, 2, 4, 1, 3, 5, 6))]
    select_n x2 -> x0, other arithmetic: 2.27 us -> none  [the longest x1 1.15 us: per_device(): inner = jnp.where(lev_index == 0, grid[1:2], grid[0:1])]
    another operation x2 -> x0, local copies, waits for them, and re-layouts: 1.82 us -> none  [the longest x1 1.38 us: to_windows(): values.reshape(levels // depth, depth, rows // WA, WA, cols // WO, WO, wi...]
  transfers between devices with their start and end apart: 6 -> 6, of which waited for: 4 -> 3; matrix products, arithmetic and copies ran while one was open for 0% -> 0% of each run, Pallas kernels for 0% -> 11%
where the time goes in v2:
time: 71.1 us; the launch traced here: 70.8 us
  starting transfers between devices  41.1 us (58%)
  Pallas kernels  14.4 us (20%)
  waiting for transfers between devices  14.1 us (20%)
  local copies, waits for them, and re-layouts  1 us (1%)
    ppermute x6, starting transfers between devices, send(): return lax.ppermute(array, AXES, route)  41.1 us
    ppermute x6, waiting for transfers between devices, send(): return lax.ppermute(array, AXES, route)  14.1 us
    pallas_call x4, Pallas kernels, run(): pl.pallas_call(kernel, out_shape=outs, in_specs=[SMEM] + [VMEM] * len(arg...  11 us
    pallas_call x1, Pallas kernels, load(): pl.pallas_call(load_kernel, out_shape=tuple((jax.ShapeDtypeStruct(a.shape...  3.39 us
  transfers between devices with their start and end apart: 6, of which 3 were waited for; matrix products, arithmetic and copies ran while one was open for 0% of the time, Pallas kernels for 11%

profile of v2, /device:TPU:1, one launch (start us, length us, event | category | flops | bytes accessed | tf_op | source)
XLA Modules:
  0.0 70.8 jit_solution(16740488977682674649)
XLA Ops:
  0.0 1.0 %dynamic-slice_bitcast_fusion = (bf16[2,72,512]{2,1,0:T(8,128)(2,1)S(1)}, bf16[2,72,512]{2,1,0:T(8,128)(2,1)S(1)}) fusion(bf16[2,2,72,512]{3,2,1,0:T(8,128)(2,1)} %bitcast.17, s32[]{:T(128)S(6)} %select_n.8, s32[]{:T(128)S(6)} %select_n.7), kind=kLoop, calls=%fused_computation | loop fusion | bytes 589832 | tf_op jit(solution)/shard_map/jit(dynamic_index_in_dim)/squeeze | solution.py:263
  1.0 21.6 %collective-permute-start.1 = (bf16[2,72,512]{2,1,0:T(8,128)(2,1)S(1)}, bf16[2,72,512]{2,1,0:T(8,128)(2,1)S(1)}, u32[]{:S(2)}, u32[]{:S(2)}) collective-permute-start(bf16[2,72,512]{2,1,0:T(8,128)(2,1)S(1)} %get-tuple-element.47), channel_id=1, source_target_pairs={{0,16},{1,17},{2,18},{3,19},{4,20},{5,21},{6,22},{7,23},{8,24},{9,... | collective-permute-start | bytes 442376 | tf_op jit(solution)/shard_map/ppermute | solution.py:27
  22.6 1.9 %collective-permute-start = (bf16[2,72,512]{2,1,0:T(8,128)(2,1)S(1)}, bf16[2,72,512]{2,1,0:T(8,128)(2,1)S(1)}, u32[]{:S(2)}, u32[]{:S(2)}) collective-permute-start(bf16[2,72,512]{2,1,0:T(8,128)(2,1)S(1)} %get-tuple-element.48), channel_id=1, source_target_pairs={{0,496},{1,497},{2,498},{3,499},{4,500},{5,501},{6,502},{7,503},{8... | collective-permute-start | bytes 442376 | tf_op jit(solution)/shard_map/ppermute | solution.py:27
  24.6 3.4 %load.1 = (bf16[2,144,512]{2,1,0:T(8,128)(2,1)S(1)}, bf16[288,288]{1,0:T(8,128)(2,1)S(1)}, bf16[72,144]{1,0:T(8,128)(2,1)S(1)}, bf16[72,144]{1,0:T(8,128)(2,1)S(...) custom-call(bf16[2,144,512]{2,1,0:T(8,128)(2,1)} %bitcast.18, ...), custom_call_target="tpu_custom_call" | custom-call | tf_op jit(solution)/shard_map/load/pallas_call | solution.py:69
  28.0 0.1 pad_add_fusion.lev_ref.place_ref
  28.1 0.0 collective-permute-done.1.second_ref
  28.1 7.8 %collective-permute-done.first_ref = bf16[2,72,512]{2,1,0:T(8,128)(2,1)S(1)} collective-permute-done((bf16[2,72,512]{2,1,0:T(8,128)(2,1)S(1)}, bf16[2,72,512]{2,1,0:T(8,128)(2,1)S(1)}, u32[]{:S(2)}, u32[]{:S(2)}) %collective-permute-start) | collective-permute-done | bytes 147488 | tf_op jit(solution)/shard_map/ppermute | solution.py:27
  35.8 1.0 %shard_map.145 = (bf16[216,512]{1,0:T(8,128)(2,1)S(1)}, bf16[216,512]{1,0:T(8,128)(2,1)S(1)}, bf16[144,512]{1,0:T(8,128)(2,1)S(1)}, bf16[72,512]{1,0:T(8,128)(2,1)S(1)}) custom-call(s32[3]{0:T(128)S(1)} %pad_add_fusion.lev_ref.place_ref, bf16[288,288]{1,0:T(8,128)(2,1)S(1)} %get-tuple-element.26.pick_ref, ...), custom_call_target="tpu_custom_call" | custom-call | tf_op jit(solution)/shard_map/pallas_call | solution.py:232
  36.9 2.9 %collective-permute-start.2 = (bf16[216,512]{1,0:T(8,128)(2,1)S(1)}, bf16[216,512]{1,0:T(8,128)(2,1)S(1)}, u32[]{:S(2)}, u32[]{:S(2)}) collective-permute-start(bf16[216,512]{1,0:T(8,128)(2,1)S(1)} %get-tuple-element.29.paired_ref), channel_id=1, source_target_pairs={{0,512},{1,513},{2,514},{3,515},{4,516},{5,517},{6,518},{7,519},{8... | collective-permute-start | bytes 663560 | tf_op jit(solution)/shard_map/ppermute | solution.py:27
  39.8 9.6 %collective-permute-start.3 = (bf16[144,512]{1,0:T(8,128)(2,1)S(1)}, bf16[144,512]{1,0:T(8,128)(2,1)S(1)}, u32[]{:S(2)}, u32[]{:S(2)}) collective-permute-start(bf16[144,512]{1,0:T(8,128)(2,1)S(1)} %get-tuple-element.30), channel_id=1, source_target_pairs={{0,15},{1,0},{2,1},{3,2},{4,3},{5,4},{6,5},{7,6},{8,7},{9,8},{10,9... | collective-permute-start | bytes 442376 | tf_op jit(solution)/shard_map/ppermute | solution.py:27
  49.4 3.1 %collective-permute-start.4 = (bf16[72,512]{1,0:T(8,128)(2,1)S(1)}, bf16[72,512]{1,0:T(8,128)(2,1)S(1)}, u32[]{:S(2)}, u32[]{:S(2)}) collective-permute-start(bf16[72,512]{1,0:T(8,128)(2,1)S(1)} %get-tuple-element.31), channel_id=1, source_target_pairs={{0,527},{1,512},{2,513},{3,514},{4,515},{5,516},{6,517},{7,518},{8... | collective-permute-start | bytes 221192 | tf_op jit(solution)/shard_map/ppermute | solution.py:27
  52.5 3.5 %collective-permute-done.4.cross_ref = bf16[72,512]{1,0:T(8,128)(2,1)S(1)} collective-permute-done((bf16[72,512]{1,0:T(8,128)(2,1)S(1)}, bf16[72,512]{1,0:T(8,128)(2,1)S(1)}, u32[]{:S(2)}, u32[]{:S(2)}) %collective-permute-start.4) | collective-permute-done | bytes 73760 | tf_op jit(solution)/shard_map/ppermute | solution.py:27
  56.0 0.0 collective-permute-done.3.east_ref
  56.0 0.0 collective-permute-done.2.other_ref
  56.0 4.3 %shard_map.146 = (bf16[144,512]{1,0:T(8,128)(2,1)S(1)}, bf16[72,512]{1,0:T(8,128)(2,1)S(1)}) custom-call(s32[3]{0:T(128)S(1)} %pad_add_fusion.lev_ref.place_ref, bf16[216,512]{1,0:T(8,128)(2,1)S(1)} %get-tuple-element.28.alone_ref, bf16[216,512]{1,0:T(8,128)(2,1)S(1)} %get-tuple-element.29.paired_ref, bf16[216,512]{1,0:T(8,128)(2,1)S(1)} %collective-permute-done.2.other_ref, ...), custom_call_target="tpu_custom_call" | custom-call | tf_op jit(solution)/shard_map/pallas_call | solution.py:232
  60.3 1.9 %collective-permute-start.5 = (bf16[72,512]{1,0:T(8,128)(2,1)S(1)}, bf16[72,512]{1,0:T(8,128)(2,1)S(1)}, u32[]{:S(2)}, u32[]{:S(2)}) collective-permute-start(bf16[72,512]{1,0:T(8,128)(2,1)S(1)} %get-tuple-element.45), channel_id=1, source_target_pairs={{0,1},{1,2},{2,3},{3,4},{4,5},{5,6},{6,7},{7,8},{8,9},{9,10},{10,1... | collective-permute-start | bytes 221192 | tf_op jit(solution)/shard_map/ppermute | solution.py:27
  62.2 4.3 %shard_map.147.partial_ref = bf16[2,144,512]{2,1,0:T(8,128)(2,1)S(1)} custom-call(s32[3]{0:T(128)S(1)} %pad_add_fusion.lev_ref.place_ref, bf16[216,512]{1,0:T(8,128)(2,1)S(1)} %get-tuple-element.28.alone_ref, bf16[216,512]{1,0:T(8,128)(2,1)S(1)} %get-tuple-element.29.paired_ref, bf16[216,512]{1,0:T(8,128)(2,1)S(1)} %collective-permute-done.2.other_ref, ...), custom_call_target="tpu_custom_call" | custom-call | tf_op jit(solution)/shard_map/pallas_call | solution.py:232
  66.5 2.8 %collective-permute-done.5.returned_ref = bf16[72,512]{1,0:T(8,128)(2,1)S(1)} collective-permute-done((bf16[72,512]{1,0:T(8,128)(2,1)S(1)}, bf16[72,512]{1,0:T(8,128)(2,1)S(1)}, u32[]{:S(2)}, u32[]{:S(2)}) %collective-permute-start.5) | collective-permute-done | bytes 73760 | tf_op jit(solution)/shard_map/ppermute | solution.py:27
  69.3 1.5 %shard_map.148 = bf16[2,144,512]{2,1,0:T(8,128)(2,1)} custom-call(s32[3]{0:T(128)S(1)} %pad_add_fusion.lev_ref.place_ref, bf16[2,144,512]{2,1,0:T(8,128)(2,1)S(1)} %shard_map.147.partial_ref, bf16[72,512]{1,0:T(8,128)(2,1)S(1)} %collective-permute-done.5.returned_ref, bf16[288,72]{1,0:T(8,128)(2,1)S(1)} %get-tuple-element.46.returned_to_ref), custom_call_target="tpu_custom_call" | custom-call | tf_op jit(solution)/shard_map/pallas_call | solution.py:232
Async XLA Ops:
  1.0 27.1 %collective-permute-start.1 = (bf16[2,72,512]{2,1,0:T(8,128)(2,1)S(1)}, bf16[2,72,512]{2,1,0:T(8,128)(2,1)S(1)}, u32[]{:S(2)}, u32[]{:S(2)}) collective-permute-start(bf16[2,72,512]{2,1,0:T(8,128)(2,1)S(1)} %get-tuple-element.47), channel_id=1, source_target_pairs={{0,16},{1,17},{2,18},{3,19},{4,20},{5,21},{6,22},{7,23},{8,24},{9,... | collective-permute-start | bytes 442376 | tf_op jit(solution)/shard_map/ppermute | solution.py:27
  22.6 13.2 %collective-permute-start = (bf16[2,72,512]{2,1,0:T(8,128)(2,1)S(1)}, bf16[2,72,512]{2,1,0:T(8,128)(2,1)S(1)}, u32[]{:S(2)}, u32[]{:S(2)}) collective-permute-start(bf16[2,72,512]{2,1,0:T(8,128)(2,1)S(1)} %get-tuple-element.48), channel_id=1, source_target_pairs={{0,496},{1,497},{2,498},{3,499},{4,500},{5,501},{6,502},{7,503},{8... | collective-permute-start | bytes 442376 | tf_op jit(solution)/shard_map/ppermute | solution.py:27
  36.9 19.2 %collective-permute-start.2 = (bf16[216,512]{1,0:T(8,128)(2,1)S(1)}, bf16[216,512]{1,0:T(8,128)(2,1)S(1)}, u32[]{:S(2)}, u32[]{:S(2)}) collective-permute-start(bf16[216,512]{1,0:T(8,128)(2,1)S(1)} %get-tuple-element.29.paired_ref), channel_id=1, source_target_pairs={{0,512},{1,513},{2,514},{3,515},{4,516},{5,517},{6,518},{7,519},{8... | collective-permute-start | bytes 663560 | tf_op jit(solution)/shard_map/ppermute | solution.py:27
  39.8 16.2 %collective-permute-start.3 = (bf16[144,512]{1,0:T(8,128)(2,1)S(1)}, bf16[144,512]{1,0:T(8,128)(2,1)S(1)}, u32[]{:S(2)}, u32[]{:S(2)}) collective-permute-start(bf16[144,512]{1,0:T(8,128)(2,1)S(1)} %get-tuple-element.30), channel_id=1, source_target_pairs={{0,15},{1,0},{2,1},{3,2},{4,3},{5,4},{6,5},{7,6},{8,7},{9,8},{10,9... | collective-permute-start | bytes 442376 | tf_op jit(solution)/shard_map/ppermute | solution.py:27
  49.4 6.7 %collective-permute-start.4 = (bf16[72,512]{1,0:T(8,128)(2,1)S(1)}, bf16[72,512]{1,0:T(8,128)(2,1)S(1)}, u32[]{:S(2)}, u32[]{:S(2)}) collective-permute-start(bf16[72,512]{1,0:T(8,128)(2,1)S(1)} %get-tuple-element.31), channel_id=1, source_target_pairs={{0,527},{1,512},{2,513},{3,514},{4,515},{5,516},{6,517},{7,518},{8... | collective-permute-start | bytes 221192 | tf_op jit(solution)/shard_map/ppermute | solution.py:27
  60.3 9.0 %collective-permute-start.5 = (bf16[72,512]{1,0:T(8,128)(2,1)S(1)}, bf16[72,512]{1,0:T(8,128)(2,1)S(1)}, u32[]{:S(2)}, u32[]{:S(2)}) collective-permute-start(bf16[72,512]{1,0:T(8,128)(2,1)S(1)} %get-tuple-element.45), channel_id=1, source_target_pairs={{0,1},{1,2},{2,3},{3,4},{4,5},{5,6},{6,7},{7,8},{8,9},{9,10},{10,1... | collective-permute-start | bytes 221192 | tf_op jit(solution)/shard_map/ppermute | solution.py:27

commit v3 on v2

--- a/solution.py
+++ b/solution.py
@@ -9,6 +9,7 @@
 
 WA = 6
 WO = 12
+HALF = WA // 2
 EDGE = WO // 2
 LOG2E = 1.4426950408889634
 AXES = ("lev", "lat", "lon")
@@ -27,32 +28,92 @@
     return lax.ppermute(array, AXES, route)
 
 
-def column_group(cols, first, last):
-    own = [r * cols + c for r in range(WA) for c in range(first, last)]
-    halo = [WA * cols + r * cols + c for r in range(WA) for c in range(first, last)]
-    return own + halo
-
-
 def one_hot(indices, size):
     table = np.zeros((len(indices), size), np.float32)
     for row, index in enumerate(indices):
         if index >= 0:
             table[row, index] = 1
-    return jnp.asarray(table, jnp.bfloat16)
-
-
-def gather_kernel(lev_ref, pick_ref, own_ref, first_ref, second_ref, alone_ref, paired_ref, west_ref, cross_ref):
+    return table
+
+
+def padded(indices, size):
+    return indices + [-1] * (size - len(indices))
+
+
+def block(cols, level, first_row, rows, first_col, last_col):
+    return [(level * WA + r) * cols + c for r in range(first_row, first_row + rows) for c in range(first_col, last_col)]
+
+
+def rounded(size):
+    return -(-size // 8) * 8
+
+
+def split_picks(levels, cols):
+    side = rounded(HALF * (cols - EDGE))
+    corner = rounded(levels * HALF * EDGE)
+    picks = []
+    for lev in range(2):
+        rows = []
+        for start in (HALF * lev, HALF * (1 - lev)):
+            for level in range(levels):
+                rows += padded(block(cols, level, start, HALF, EDGE, cols), side)
+        for start in (HALF * lev, HALF * (1 - lev)):
+            rows += padded([t for level in range(levels) for t in block(cols, level, start, HALF, 0, EDGE)], corner)
+        rows += [t for level in range(levels) for t in block(cols, level, 0, WA, 0, EDGE)]
+        picks.append(one_hot(rows, levels * WA * cols))
+    return np.stack(picks)
+
+
+def gather_picks(levels, cols):
+    own = WA * cols
+    wide = cols - EDGE
+    side = rounded(HALF * wide)
+    corner = rounded(levels * HALF * EDGE)
+    first, second = own, own + side
+    corners = own + 2 * side
+    east = corners + 2 * corner
+    picks = []
+    for level in range(levels):
+        def halo(first_col, last_col):
+            return [at + r * wide + c for at in (first, second) for r in range(HALF) for c in range(first_col, last_col)]
+
+        cells = HALF * EDGE
+        rows = block(cols, 0, 0, WA, EDGE, EDGE + WO) + halo(0, WO)
+        rows += [east + level * 2 * cells + t for t in range(2 * cells)]
+        rows += block(cols, 0, 0, WA, EDGE + WO, cols) + halo(WO, wide)
+        rows += [corners + which * corner + level * cells + t for which in range(2) for t in range(cells)]
+        picks.append(one_hot(rows, east + levels * 2 * cells))
+    return np.stack(picks)
+
+
+def split_kernel(lev_ref, pick_ref, grid_ref, own_ref, first_ref, second_ref, corner_ref, corner_2_ref, west_ref, held, sems):
+    copies = [
+        pltpu.make_async_copy(grid_ref, own_ref, sems.at[0]),
+        pltpu.make_async_copy(pick_ref.at[lev_ref[0]], held, sems.at[1]),
+    ]
+    for copy in copies:
+        copy.start()
+    for copy in copies:
+        copy.wait()
+    levels, own, width = own_ref.shape
+    picked = jnp.dot(held[...], own_ref[...].reshape(levels * own, width), preferred_element_type=jnp.float32)
+    picked = picked.astype(jnp.bfloat16)
+    at = 0
+    for ref in (first_ref, second_ref):
+        for level in range(levels):
+            ref[level] = picked[at : at + ref.shape[1]]
+            at += ref.shape[1]
+    for ref in (corner_ref, corner_2_ref, west_ref):
+        ref[...] = picked[at : at + ref.shape[0]]
+        at += ref.shape[0]
+
+
+def gather_kernel(lev_ref, pick_ref, own_ref, first_ref, second_ref, corner_ref, corner_2_ref, east_ref, alone_ref, paired_ref):
     lev = lev_ref[0]
-    kept = alone_ref.shape[0]
-    edge = cross_ref.shape[0]
-    for i, (level, out_ref) in enumerate(((lev, alone_ref), (1 - lev, paired_ref))):
-        source = jnp.concatenate([own_ref[level], first_ref[level], second_ref[level]], 0)
-        picked = jnp.dot(pick_ref[...], source, preferred_element_type=jnp.float32)
-        picked = picked.astype(jnp.bfloat16)
-        out_ref[...] = picked[:kept]
-        west_ref[i * edge : (i + 1) * edge, :] = picked[kept:]
-        if i == 1:
-            cross_ref[...] = picked[kept:]
+    for level, out_ref in ((lev, alone_ref), (1 - lev, paired_ref)):
+        source = [own_ref[level], first_ref[level], second_ref[level], corner_ref[...], corner_2_ref[...], east_ref[...]]
+        picked = jnp.dot(pick_ref[level], jnp.concatenate(source, 0), preferred_element_type=jnp.float32)
+        out_ref[...] = picked.astype(jnp.bfloat16)
 
 
 def load_kernel(*refs):
@@ -128,22 +189,20 @@
     return jnp.concatenate(parts, 1)
 
 
-def allowed_keys(place_ref, queries, group, swapped):
+def allowed_keys(place_ref, queries, period, swapped):
     lev = place_ref[0]
     shape = (queries, 2 * queries)
     row = lax.broadcasted_iota(jnp.int32, shape, 0)
     col = lax.broadcasted_iota(jnp.int32, shape, 1)
-    row = lax.rem(row, group)
-    col = lax.rem(col, 2 * group)
-    quarter = group // 2
-    q_half = jnp.where(row < quarter, 0, 1)
+    q_half = jnp.where(lax.rem(row, period) < period // 2, 0, 1)
+    part = jnp.where(lax.rem(col, period) < period // 2, 0, 1)
     first = lev if swapped else 1 - lev
-    k_half = jnp.where(col < quarter, 0, jnp.where(col < 2 * quarter, 1, jnp.where(col < 3 * quarter, first, 1 - first)))
+    k_half = jnp.where(col < queries, part, jnp.where(part == 0, first, 1 - first))
     closed = jnp.where(k_half == 0, place_ref[1], place_ref[2])
-    return jnp.where((q_half == k_half) & ((col < group) | (closed == 0)), 1.0, 0.0)
-
-
-def run_windows(sources, query, place_ref, group, heads_ref, logit_ref, weights, kv_ref):
+    return jnp.where((q_half == k_half) & ((col < queries) | (closed == 0)), 1.0, 0.0)
+
+
+def run_windows(sources, query, place_ref, period, heads_ref, logit_ref, weights, kv_ref):
     qkv_ref, proj_ref, up_ref, down_ref, gain_attn_ref, gain_mlp_ref = weights
     width = proj_ref.shape[0]
     tokens = kv_ref.shape[0]
@@ -152,8 +211,8 @@
     kv = jnp.dot(sources, qkv_ref[:, width:], preferred_element_type=jnp.float32)
     kv_ref[...] = kv.astype(jnp.bfloat16)
     q = jnp.dot(query, qkv_ref[:, :width], preferred_element_type=jnp.float32).astype(jnp.bfloat16)
-    own = allowed_keys(place_ref, count, group, False)
-    other = allowed_keys(place_ref, count, group, True)
+    own = allowed_keys(place_ref, count, period, False)
+    other = allowed_keys(place_ref, count, period, True)
     logit = logit_ref[...] * LOG2E
     mixed = []
     for i, (first, last, allowed) in enumerate(((0, span, own), (span, tokens, jnp.concatenate([own, other], 1)))):
@@ -172,23 +231,15 @@
 
 
 def border_kernel(
-    place_ref, alone_ref, paired_ref, other_ref, east_ref, cross_ref, pick_ref, back_ref, heads_ref, logit_ref,
+    place_ref, alone_ref, paired_ref, other_ref, back_ref, heads_ref, logit_ref,
     qkv_ref, proj_ref, up_ref, down_ref, gain_attn_ref, gain_mlp_ref, out_ref, return_ref, kv_ref,
 ):
-    edge = cross_ref.shape[0]
-    start = alone_ref.shape[0] - edge
-    pieces = (
-        alone_ref[start:, :], east_ref[:edge, :], paired_ref[start:, :], east_ref[edge:, :],
-        other_ref[start:, :], cross_ref[...],
-    )
-    sources = jnp.concatenate(pieces, 0)
-    query = [
-        jnp.dot(pick_ref[...], sources[i * 2 * edge : (i + 1) * 2 * edge], preferred_element_type=jnp.float32)
-        for i in range(2)
-    ]
-    query = jnp.concatenate(query, 0).astype(jnp.bfloat16)
+    span = kv_ref.shape[0] // 3
+    count = span // 2
+    sources = jnp.concatenate([alone_ref[span:, :], paired_ref[span:, :], other_ref[span:, :]], 0)
+    query = jnp.concatenate([alone_ref[span : span + count, :], paired_ref[span : span + count, :]], 0)
     weights = (qkv_ref, proj_ref, up_ref, down_ref, gain_attn_ref, gain_mlp_ref)
-    result = run_windows(sources, query, place_ref, edge // 2, heads_ref, logit_ref, weights, kv_ref)
+    result = run_windows(sources, query, place_ref, count // 2, heads_ref, logit_ref, weights, kv_ref)
     out_ref[...] = result
     back = jnp.dot(back_ref[...], result, preferred_element_type=jnp.float32)
     return_ref[...] = back.astype(jnp.bfloat16)
@@ -244,7 +295,6 @@
 def per_device(grid, w_qkv, w_proj, w_up, w_down, logit_scale, gain_attn, gain_mlp):
     levels, rows, cols, width = grid.shape
     own = rows * cols
-    half = own // 2
     edge = 2 * WA * EDGE
     heads = logit_scale.shape[0]
     bf16 = jnp.bfloat16
@@ -257,39 +307,52 @@
     last = lax.axis_size("lat") - 1
     place = jnp.stack([lev, (lat == 0).astype(jnp.int32), (lat == last).astype(jnp.int32)])
 
-    tokens = grid.reshape(levels, own, width)
-    halves = grid.reshape(levels, 2, half, width)
-    sent_first = lax.dynamic_index_in_dim(halves, lev, 1, keepdims=False)
-    sent_second = lax.dynamic_index_in_dim(halves, 1 - lev, 1, keepdims=False)
-    first = send(sent_first, lambda c, i, j: (c, i + 2 * c - 1, j))
-    second = send(sent_second, lambda c, i, j: (c, i + 1 - 2 * c, j))
-
-    groups = column_group(cols, EDGE, EDGE + WO) + column_group(cols, EDGE + WO, cols) + column_group(cols, 0, EDGE)
+    side = rounded(HALF * (cols - EDGE))
+    corner = rounded(levels * HALF * EDGE)
+    outs = (
+        shape(levels, own, width), shape(levels, side, width), shape(levels, side, width),
+        shape(corner, width), shape(corner, width), shape(edge, width),
+    )
+    picks = split_picks(levels, cols)
+    in_hbm = pl.BlockSpec(memory_space=pltpu.HBM)
+    held = [pltpu.VMEM(picks.shape[1:], bf16), pltpu.SemaphoreType.DMA((2,))]
+    tokens, first, second, corner_1, corner_2, west = pl.pallas_call(
+        split_kernel, out_shape=outs, in_specs=[SMEM, in_hbm, in_hbm], out_specs=(VMEM,) * len(outs), scratch_shapes=held,
+        compiler_params=pltpu.CompilerParams(vmem_limit_bytes=8 << 20), name="split",
+    )(
+        lev.reshape(1), pltpu.with_memory_space_constraint(jnp.asarray(picks, bf16), pltpu.HBM),
+        pltpu.with_memory_space_constraint(grid.reshape(levels, own, width), pltpu.HBM),
+    )
+    first = send(first, lambda c, i, j: (c, i + 2 * c - 1, j))
+    corner_1 = send(corner_1, lambda c, i, j: (c, i + 2 * c - 1, j - 1))
+    east = send(west, lambda c, i, j: (c, i, j - 1))
+    second = send(second, lambda c, i, j: (c, i + 1 - 2 * c, j))
+    corner_2 = send(corner_2, lambda c, i, j: (c, i + 1 - 2 * c, j - 1))
+
     heads_of = jnp.asarray(np.repeat(np.eye(heads, dtype=np.float32), width // heads, axis=1), bf16)
     quarter = edge // 2
     spots = [(r, c) for r in range(rows) for c in range(cols)]
-    pick = [edge + t for t in range(quarter)] + list(range(quarter))
     back = [i * edge + t for i in range(2) for t in range(quarter)]
     middle_to = [r * WO + c - EDGE if EDGE <= c < EDGE + WO else -1 for r, c in spots]
     border_to = [quarter + r * EDGE + c - EDGE - WO if c >= EDGE + WO else -1 for r, c in spots]
     returned_to = [i * quarter + r * EDGE + c if c < EDGE else -1 for i in range(2) for r, c in spots]
-    tokens, groups, pick, back, middle_to, border_to, returned_to, *shared = load(
-        tokens, one_hot(groups, 2 * own), one_hot(pick, 2 * edge), one_hot(back, 2 * edge), one_hot(middle_to, edge),
-        one_hot(border_to, edge), one_hot(returned_to, edge),
+    tables = [
+        gather_picks(levels, cols), one_hot(back, 2 * edge), one_hot(middle_to, edge), one_hot(border_to, edge),
+        one_hot(returned_to, edge),
+    ]
+    groups, back, middle_to, border_to, returned_to, *shared = load(
+        *(jnp.asarray(table, bf16) for table in tables),
         heads_of, logit_scale.reshape(1, heads), w_qkv, w_proj, w_up, w_down,
         gain_attn.reshape(1, width), gain_mlp.reshape(1, width),
     )
 
-    kept = 2 * own - edge
-    outs = (shape(kept, width), shape(kept, width), shape(2 * edge, width), shape(edge, width))
-    alone, paired, west, west_paired = call(gather_kernel, outs, 8)(place, groups, tokens, first, second)
-    east = send(west, lambda c, i, j: (c, i, j - 1))
-    cross = send(west_paired, lambda c, i, j: (1 - c, i, j - 1))
+    outs = (shape(4 * edge, width), shape(4 * edge, width))
+    alone, paired = call(gather_kernel, outs, 8)(place, groups, tokens, first, second, corner_1, corner_2, east)
     other = send(paired, lambda c, i, j: (1 - c, i, j))
 
     kv = [pltpu.VMEM((6 * edge, 2 * width), bf16)]
     border, returning = call(border_kernel, (shape(2 * edge, width), shape(edge, width)), 16, kv)(
-        place, alone, paired, other, east, cross, pick, back, *shared
+        place, alone, paired, other, back, *shared
     )
     returned = send(returning, lambda c, i, j: (c, i, j + 1))
     partial = call(middle_kernel, shape(levels, own, width), 16, kv)(

time: 71.1 us -> 72.4 us (1.018)
  starting transfers between devices: 41.1 us -> 50.1 us
  waiting for transfers between devices: 14.1 us -> 6.03 us
  Pallas kernels: 14.4 us -> 15.7 us
  local copies, waits for them, and re-layouts: 1 us -> 0 us
    ppermute x6 -> x7, starting transfers between devices: 41.1 us -> 50.1 us  [send(): return lax.ppermute(array, AXES, route)]
    ppermute x6 -> x7, waiting for transfers between devices: 14.1 us -> 6.03 us  [send(): return lax.ppermute(array, AXES, route)]
    pallas_call x0 -> x1, Pallas kernels: none -> 1.43 us  [per_device(): pl.pallas_call(split_kernel, out_shape=outs, in_specs=[SMEM, in_hbm, in_h...]
    squeeze x1 -> x0, local copies, waits for them, and re-layouts: 1 us -> none  [per_device(): sent_second = lax.dynamic_index_in_dim(halves, 1 - lev, 1, keepdims=False)]
  transfers between devices with their start and end apart: 6 -> 7, of which waited for: 3 -> 2; matrix products, arithmetic and copies ran while one was open for 0% -> 0% of each run, Pallas kernels for 11% -> 11%
where the time goes in v3:
time: 72.4 us; the launch traced here: 72.1 us
  starting transfers between devices  50.1 us (69%)
  Pallas kernels  15.7 us (22%)
  waiting for transfers between devices  6.03 us (8%)
    ppermute x7, starting transfers between devices, send(): return lax.ppermute(array, AXES, route)  50.1 us
    pallas_call x4, Pallas kernels, run(): pl.pallas_call(kernel, out_shape=outs, in_specs=[SMEM] + [VMEM] * len(arg...  11 us
    ppermute x7, waiting for transfers between devices, send(): return lax.ppermute(array, AXES, route)  6.03 us
    pallas_call x1, Pallas kernels, load(): pl.pallas_call(load_kernel, out_shape=tuple((jax.ShapeDtypeStruct(a.shape...  3.28 us
  transfers between devices with their start and end apart: 7, of which 2 were waited for; matrix products, arithmetic and copies ran while one was open for 0% of the time, Pallas kernels for 11%

profile of v3, /device:TPU:1, one launch (start us, length us, event | category | flops | bytes accessed | tf_op | source)
XLA Modules:
  0.0 72.1 jit_solution(8304165482712296259)
XLA Ops:
  0.0 1.4 %split.1 = (bf16[2,144,512]{2,1,0:T(8,128)(2,1)S(1)}, bf16[2,56,512]{2,1,0:T(8,128)(2,1)S(1)}, bf16[2,56,512]{2,1,0:T(8,128)(2,1)S(1)}, bf16[40,512]{1,0:T(8,128...) custom-call(s32[1]{0:T(128)} %bitcast.lev_ref, bf16[2,376,288]{2,1,0:T(8,128)(2,1)} %constant.30.clone.pick_ref, ...), custom_call_target="tpu_custom_call" | custom-call | tf_op jit(solution)/shard_map/split/pallas_call | solution.py:319
  1.4 11.5 %collective-permute-start = (bf16[2,56,512]{2,1,0:T(8,128)(2,1)S(1)}, bf16[2,56,512]{2,1,0:T(8,128)(2,1)S(1)}, u32[]{:S(2)}, u32[]{:S(2)}) collective-permute-start(bf16[2,56,512]{2,1,0:T(8,128)(2,1)S(1)} %get-tuple-element.30), channel_id=1, source_target_pairs={{0,496},{1,497},{2,498},{3,499},{4,500},{5,501},{6,502},{7,503},{8... | collective-permute-start | bytes 344072 | tf_op jit(solution)/shard_map/ppermute | solution.py:28
  12.9 12.1 %collective-permute-start.1 = (bf16[2,56,512]{2,1,0:T(8,128)(2,1)S(1)}, bf16[2,56,512]{2,1,0:T(8,128)(2,1)S(1)}, u32[]{:S(2)}, u32[]{:S(2)}) collective-permute-start(bf16[2,56,512]{2,1,0:T(8,128)(2,1)S(1)} %get-tuple-element.31), channel_id=1, source_target_pairs={{0,16},{1,17},{2,18},{3,19},{4,20},{5,21},{6,22},{7,23},{8,24},{9,... | collective-permute-start | bytes 344072 | tf_op jit(solution)/shard_map/ppermute | solution.py:28
  25.0 5.4 %collective-permute-start.2 = (bf16[40,512]{1,0:T(8,128)(2,1)S(1)}, bf16[40,512]{1,0:T(8,128)(2,1)S(1)}, u32[]{:S(2)}, u32[]{:S(2)}) collective-permute-start(bf16[40,512]{1,0:T(8,128)(2,1)S(1)} %get-tuple-element.32), channel_id=1, source_target_pairs={{0,511},{1,496},{2,497},{3,498},{4,499},{5,500},{6,501},{7,502},{8... | collective-permute-start | bytes 122888 | tf_op jit(solution)/shard_map/ppermute | solution.py:28
  30.4 8.4 %collective-permute-start.3 = (bf16[40,512]{1,0:T(8,128)(2,1)S(1)}, bf16[40,512]{1,0:T(8,128)(2,1)S(1)}, u32[]{:S(2)}, u32[]{:S(2)}) collective-permute-start(bf16[40,512]{1,0:T(8,128)(2,1)S(1)} %get-tuple-element.33), channel_id=1, source_target_pairs={{0,31},{1,16},{2,17},{3,18},{4,19},{5,20},{6,21},{7,22},{8,23},{9,... | collective-permute-start | bytes 122888 | tf_op jit(solution)/shard_map/ppermute | solution.py:28
  38.8 4.9 %collective-permute-start.4 = (bf16[72,512]{1,0:T(8,128)(2,1)S(1)}, bf16[72,512]{1,0:T(8,128)(2,1)S(1)}, u32[]{:S(2)}, u32[]{:S(2)}) collective-permute-start(bf16[72,512]{1,0:T(8,128)(2,1)S(1)} %get-tuple-element.34), channel_id=1, source_target_pairs={{0,15},{1,0},{2,1},{3,2},{4,3},{5,4},{6,5},{7,6},{8,7},{9,8},{10,9... | collective-permute-start | bytes 221192 | tf_op jit(solution)/shard_map/ppermute | solution.py:28
  43.7 0.1 pad_add_fusion.lev_ref.place_ref
  43.8 3.3 %load.1 = (bf16[2,288,408]{2,1,0:T(8,128)(2,1)S(1)}, bf16[72,144]{1,0:T(8,128)(2,1)S(1)}, bf16[144,72]{1,0:T(8,128)(2,1)S(1)}, bf16[144,72]{1,0:T(8,128)(2,1)S(1...) custom-call(bf16[2,288,408]{2,1,0:T(8,128)(2,1)} %constant.32.clone., ...), custom_call_target="tpu_custom_call" | custom-call | tf_op jit(solution)/shard_map/load/pallas_call | solution.py:130
  47.1 0.0 collective-permute-done.2.corner_ref
  47.1 0.0 collective-permute-done.3.corner_2_ref
  47.1 0.0 collective-permute-done.4.east_ref
  47.1 0.0 collective-permute-done.first_ref
  47.1 0.0 collective-permute-done.1.second_ref
  47.1 1.0 %shard_map.145 = (bf16[288,512]{1,0:T(8,128)(2,1)S(1)}, bf16[288,512]{1,0:T(8,128)(2,1)S(1)}) custom-call(s32[3]{0:T(128)S(1)} %pad_add_fusion.lev_ref.place_ref, bf16[2,288,408]{2,1,0:T(8,128)(2,1)S(1)} %get-tuple-element.28.pick_ref, bf16[2,144,512]{2,1,0:T(8,128)(2,1)S(1)} %get-tuple-element.29.own_ref, ...), custom_call_target="tpu_custom_call" | custom-call | tf_op jit(solution)/shard_map/pallas_call | solution.py:283
  48.1 6.0 %collective-permute-start.5 = (bf16[288,512]{1,0:T(8,128)(2,1)S(1)}, bf16[288,512]{1,0:T(8,128)(2,1)S(1)}, u32[]{:S(2)}, u32[]{:S(2)}) collective-permute-start(bf16[288,512]{1,0:T(8,128)(2,1)S(1)} %get-tuple-element.36.paired_ref), channel_id=1, source_target_pairs={{0,512},{1,513},{2,514},{3,515},{4,516},{5,517},{6,518},{7,519},{8... | collective-permute-start | bytes 884744 | tf_op jit(solution)/shard_map/ppermute | solution.py:28
  54.1 1.2 %collective-permute-done.5.other_ref = bf16[288,512]{1,0:T(8,128)(2,1)S(1)} collective-permute-done((bf16[288,512]{1,0:T(8,128)(2,1)S(1)}, bf16[288,512]{1,0:T(8,128)(2,1)S(1)}, u32[]{:S(2)}, u32[]{:S(2)}) %collective-permute-start.5) | collective-permute-done | bytes 294944 | tf_op jit(solution)/shard_map/ppermute | solution.py:28
  55.3 4.2 %shard_map.146 = (bf16[144,512]{1,0:T(8,128)(2,1)S(1)}, bf16[72,512]{1,0:T(8,128)(2,1)S(1)}) custom-call(s32[3]{0:T(128)S(1)} %pad_add_fusion.lev_ref.place_ref, bf16[288,512]{1,0:T(8,128)(2,1)S(1)} %get-tuple-element.35.alone_ref, bf16[288,512]{1,0:T(8,128)(2,1)S(1)} %get-tuple-element.36.paired_ref, bf16[288,512]{1,0:T(8,128)(2,1)S(1)} %collective-permute-done.5.other_ref, ...), custom_call_target="tpu_custom_call" | custom-call | tf_op jit(solution)/shard_map/pallas_call | solution.py:283
  59.5 1.9 %collective-permute-start.6 = (bf16[72,512]{1,0:T(8,128)(2,1)S(1)}, bf16[72,512]{1,0:T(8,128)(2,1)S(1)}, u32[]{:S(2)}, u32[]{:S(2)}) collective-permute-start(bf16[72,512]{1,0:T(8,128)(2,1)S(1)} %get-tuple-element.49), channel_id=1, source_target_pairs={{0,1},{1,2},{2,3},{3,4},{4,5},{5,6},{6,7},{7,8},{8,9},{9,10},{10,1... | collective-permute-start | bytes 221192 | tf_op jit(solution)/shard_map/ppermute | solution.py:28
  61.4 4.3 %shard_map.147.partial_ref = bf16[2,144,512]{2,1,0:T(8,128)(2,1)S(1)} custom-call(s32[3]{0:T(128)S(1)} %pad_add_fusion.lev_ref.place_ref, bf16[288,512]{1,0:T(8,128)(2,1)S(1)} %get-tuple-element.35.alone_ref, bf16[288,512]{1,0:T(8,128)(2,1)S(1)} %get-tuple-element.36.paired_ref, bf16[288,512]{1,0:T(8,128)(2,1)S(1)} %collective-permute-done.5.other_ref, ...), custom_call_target="tpu_custom_call" | custom-call | tf_op jit(solution)/shard_map/pallas_call | solution.py:283
  65.8 4.8 %collective-permute-done.6.returned_ref = bf16[72,512]{1,0:T(8,128)(2,1)S(1)} collective-permute-done((bf16[72,512]{1,0:T(8,128)(2,1)S(1)}, bf16[72,512]{1,0:T(8,128)(2,1)S(1)}, u32[]{:S(2)}, u32[]{:S(2)}) %collective-permute-start.6) | collective-permute-done | bytes 73760 | tf_op jit(solution)/shard_map/ppermute | solution.py:28
  70.6 1.5 %shard_map.148 = bf16[2,144,512]{2,1,0:T(8,128)(2,1)} custom-call(s32[3]{0:T(128)S(1)} %pad_add_fusion.lev_ref.place_ref, bf16[2,144,512]{2,1,0:T(8,128)(2,1)S(1)} %shard_map.147.partial_ref, bf16[72,512]{1,0:T(8,128)(2,1)S(1)} %collective-permute-done.6.returned_ref, bf16[288,72]{1,0:T(8,128)(2,1)S(1)} %get-tuple-element.50.returned_to_ref), custom_call_target="tpu_custom_call" | custom-call | tf_op jit(solution)/shard_map/pallas_call | solution.py:283
Async XLA Ops:
  1.4 45.7 %collective-permute-start = (bf16[2,56,512]{2,1,0:T(8,128)(2,1)S(1)}, bf16[2,56,512]{2,1,0:T(8,128)(2,1)S(1)}, u32[]{:S(2)}, u32[]{:S(2)}) collective-permute-start(bf16[2,56,512]{2,1,0:T(8,128)(2,1)S(1)} %get-tuple-element.30), channel_id=1, source_target_pairs={{0,496},{1,497},{2,498},{3,499},{4,500},{5,501},{6,502},{7,503},{8... | collective-permute-start | bytes 344072 | tf_op jit(solution)/shard_map/ppermute | solution.py:28
  12.9 34.2 %collective-permute-start.1 = (bf16[2,56,512]{2,1,0:T(8,128)(2,1)S(1)}, bf16[2,56,512]{2,1,0:T(8,128)(2,1)S(1)}, u32[]{:S(2)}, u32[]{:S(2)}) collective-permute-start(bf16[2,56,512]{2,1,0:T(8,128)(2,1)S(1)} %get-tuple-element.31), channel_id=1, source_target_pairs={{0,16},{1,17},{2,18},{3,19},{4,20},{5,21},{6,22},{7,23},{8,24},{9,... | collective-permute-start | bytes 344072 | tf_op jit(solution)/shard_map/ppermute | solution.py:28
  25.0 22.1 %collective-permute-start.2 = (bf16[40,512]{1,0:T(8,128)(2,1)S(1)}, bf16[40,512]{1,0:T(8,128)(2,1)S(1)}, u32[]{:S(2)}, u32[]{:S(2)}) collective-permute-start(bf16[40,512]{1,0:T(8,128)(2,1)S(1)} %get-tuple-element.32), channel_id=1, source_target_pairs={{0,511},{1,496},{2,497},{3,498},{4,499},{5,500},{6,501},{7,502},{8... | collective-permute-start | bytes 122888 | tf_op jit(solution)/shard_map/ppermute | solution.py:28
  30.4 16.7 %collective-permute-start.3 = (bf16[40,512]{1,0:T(8,128)(2,1)S(1)}, bf16[40,512]{1,0:T(8,128)(2,1)S(1)}, u32[]{:S(2)}, u32[]{:S(2)}) collective-permute-start(bf16[40,512]{1,0:T(8,128)(2,1)S(1)} %get-tuple-element.33), channel_id=1, source_target_pairs={{0,31},{1,16},{2,17},{3,18},{4,19},{5,20},{6,21},{7,22},{8,23},{9,... | collective-permute-start | bytes 122888 | tf_op jit(solution)/shard_map/ppermute | solution.py:28
  38.8 8.3 %collective-permute-start.4 = (bf16[72,512]{1,0:T(8,128)(2,1)S(1)}, bf16[72,512]{1,0:T(8,128)(2,1)S(1)}, u32[]{:S(2)}, u32[]{:S(2)}) collective-permute-start(bf16[72,512]{1,0:T(8,128)(2,1)S(1)} %get-tuple-element.34), channel_id=1, source_target_pairs={{0,15},{1,0},{2,1},{3,2},{4,3},{5,4},{6,5},{7,6},{8,7},{9,8},{10,9... | collective-permute-start | bytes 221192 | tf_op jit(solution)/shard_map/ppermute | solution.py:28
  48.1 7.2 %collective-permute-start.5 = (bf16[288,512]{1,0:T(8,128)(2,1)S(1)}, bf16[288,512]{1,0:T(8,128)(2,1)S(1)}, u32[]{:S(2)}, u32[]{:S(2)}) collective-permute-start(bf16[288,512]{1,0:T(8,128)(2,1)S(1)} %get-tuple-element.36.paired_ref), channel_id=1, source_target_pairs={{0,512},{1,513},{2,514},{3,515},{4,516},{5,517},{6,518},{7,519},{8... | collective-permute-start | bytes 884744 | tf_op jit(solution)/shard_map/ppermute | solution.py:28
  59.5 11.1 %collective-permute-start.6 = (bf16[72,512]{1,0:T(8,128)(2,1)S(1)}, bf16[72,512]{1,0:T(8,128)(2,1)S(1)}, u32[]{:S(2)}, u32[]{:S(2)}) collective-permute-start(bf16[72,512]{1,0:T(8,128)(2,1)S(1)} %get-tuple-element.49), channel_id=1, source_target_pairs={{0,1},{1,2},{2,3},{3,4},{4,5},{5,6},{6,7},{7,8},{8,9},{9,10},{10,1... | collective-permute-start | bytes 221192 | tf_op jit(solution)/shard_map/ppermute | solution.py:28

commit v4 on v2

--- a/solution.py
+++ b/solution.py
@@ -128,8 +128,8 @@
     return jnp.concatenate(parts, 1)
 
 
-def allowed_keys(place_ref, queries, group, swapped):
-    lev = place_ref[0]
+def allowed_keys(place_ref, queries, group):
+    first = place_ref[3]
     shape = (queries, 2 * queries)
     row = lax.broadcasted_iota(jnp.int32, shape, 0)
     col = lax.broadcasted_iota(jnp.int32, shape, 1)
@@ -137,7 +137,6 @@
     col = lax.rem(col, 2 * group)
     quarter = group // 2
     q_half = jnp.where(row < quarter, 0, 1)
-    first = lev if swapped else 1 - lev
     k_half = jnp.where(col < quarter, 0, jnp.where(col < 2 * quarter, 1, jnp.where(col < 3 * quarter, first, 1 - first)))
     closed = jnp.where(k_half == 0, place_ref[1], place_ref[2])
     return jnp.where((q_half == k_half) & ((col < group) | (closed == 0)), 1.0, 0.0)
@@ -152,11 +151,10 @@
     kv = jnp.dot(sources, qkv_ref[:, width:], preferred_element_type=jnp.float32)
     kv_ref[...] = kv.astype(jnp.bfloat16)
     q = jnp.dot(query, qkv_ref[:, :width], preferred_element_type=jnp.float32).astype(jnp.bfloat16)
-    own = allowed_keys(place_ref, count, group, False)
-    other = allowed_keys(place_ref, count, group, True)
+    own = allowed_keys(place_ref, count, group)
     logit = logit_ref[...] * LOG2E
     mixed = []
-    for i, (first, last, allowed) in enumerate(((0, span, own), (span, tokens, jnp.concatenate([own, other], 1)))):
+    for i, (first, last, allowed) in enumerate(((0, span, own), (span, tokens, jnp.concatenate([own, own], 1)))):
         keys = kv_ref[first:last, :width]
         values = kv_ref[first:last, width:]
         mixed.append(attend(q[i * count : (i + 1) * count], keys, values, allowed, logit, heads_ref[...]))
@@ -255,14 +253,15 @@
     lev = lax.axis_index("lev").astype(jnp.int32)
     lat = lax.axis_index("lat")
     last = lax.axis_size("lat") - 1
-    place = jnp.stack([lev, (lat == 0).astype(jnp.int32), (lat == last).astype(jnp.int32)])
+    place = jnp.stack([lev, (lat == 0).astype(jnp.int32), (lat == last).astype(jnp.int32), lax.rem(lat, 2).astype(jnp.int32)])
 
     tokens = grid.reshape(levels, own, width)
     halves = grid.reshape(levels, 2, half, width)
-    sent_first = lax.dynamic_index_in_dim(halves, lev, 1, keepdims=False)
-    sent_second = lax.dynamic_index_in_dim(halves, 1 - lev, 1, keepdims=False)
-    first = send(sent_first, lambda c, i, j: (c, i + 2 * c - 1, j))
-    second = send(sent_second, lambda c, i, j: (c, i + 1 - 2 * c, j))
+    odd = lax.rem(lat, 2).astype(jnp.int32)
+    sent_first = lax.dynamic_index_in_dim(halves, odd, 1, keepdims=False)
+    sent_second = lax.dynamic_index_in_dim(halves, 1 - odd, 1, keepdims=False)
+    first = send(sent_first, lambda c, i, j: (c, i - 1 + 2 * (i % 2), j))
+    second = send(sent_second, lambda c, i, j: (c, i + 1 - 2 * (i % 2), j))
 
     groups = column_group(cols, EDGE, EDGE + WO) + column_group(cols, EDGE + WO, cols) + column_group(cols, 0, EDGE)
     heads_of = jnp.asarray(np.repeat(np.eye(heads, dtype=np.float32), width // heads, axis=1), bf16)

time: 71.1 us -> 71.3 us (level)
  waiting for transfers between devices: 14.1 us -> 15 us
    ppermute x6, waiting for transfers between devices: 14.1 us -> 15 us  [send(): return lax.ppermute(array, AXES, route)]
where the time goes in v4:
time: 71.3 us; the launch traced here: 71 us
  starting transfers between devices  40.4 us (57%)
  waiting for transfers between devices  15 us (21%)
  Pallas kernels  14.4 us (20%)
  local copies, waits for them, and re-layouts  1 us (1%)
    ppermute x6, starting transfers between devices, send(): return lax.ppermute(array, AXES, route)  40.4 us
    ppermute x6, waiting for transfers between devices, send(): return lax.ppermute(array, AXES, route)  15 us
    pallas_call x4, Pallas kernels, run(): pl.pallas_call(kernel, out_shape=outs, in_specs=[SMEM] + [VMEM] * len(arg...  11 us
    pallas_call x1, Pallas kernels, load(): pl.pallas_call(load_kernel, out_shape=tuple((jax.ShapeDtypeStruct(a.shape...  3.39 us
  transfers between devices with their start and end apart: 6, of which 3 were waited for; matrix products, arithmetic and copies ran while one was open for 0% of the time, Pallas kernels for 11%

profile of v4, /device:TPU:1, one launch (start us, length us, event | category | flops | bytes accessed | tf_op | source)
XLA Modules:
  0.0 71.0 jit_solution(14591231941475521025)
XLA Ops:
  0.0 1.0 %dynamic-slice_bitcast_fusion = (bf16[2,72,512]{2,1,0:T(8,128)(2,1)S(1)}, bf16[2,72,512]{2,1,0:T(8,128)(2,1)S(1)}) fusion(bf16[2,2,72,512]{3,2,1,0:T(8,128)(2,1)} %bitcast.18, s32[]{:T(128)S(6)} %select_n.8, s32[]{:T(128)S(6)} %select_n.7), kind=kLoop, calls=%fused_computation | loop fusion | bytes 589832 | tf_op jit(solution)/shard_map/jit(dynamic_index_in_dim)/squeeze | solution.py:262
  1.0 11.5 %collective-permute-start.1 = (bf16[2,72,512]{2,1,0:T(8,128)(2,1)S(1)}, bf16[2,72,512]{2,1,0:T(8,128)(2,1)S(1)}, u32[]{:S(2)}, u32[]{:S(2)}) collective-permute-start(bf16[2,72,512]{2,1,0:T(8,128)(2,1)S(1)} %get-tuple-element.47), channel_id=1, source_target_pairs={{0,16},{1,17},{2,18},{3,19},{4,20},{5,21},{6,22},{7,23},{8,24},{9,... | collective-permute-start | bytes 442376 | tf_op jit(solution)/shard_map/ppermute | solution.py:27
  12.5 13.5 %collective-permute-start = (bf16[2,72,512]{2,1,0:T(8,128)(2,1)S(1)}, bf16[2,72,512]{2,1,0:T(8,128)(2,1)S(1)}, u32[]{:S(2)}, u32[]{:S(2)}) collective-permute-start(bf16[2,72,512]{2,1,0:T(8,128)(2,1)S(1)} %get-tuple-element.48), channel_id=1, source_target_pairs={{0,496},{1,497},{2,498},{3,499},{4,500},{5,501},{6,502},{7,503},{8... | collective-permute-start | bytes 442376 | tf_op jit(solution)/shard_map/ppermute | solution.py:27
  26.0 3.4 %load.1 = (bf16[2,144,512]{2,1,0:T(8,128)(2,1)S(1)}, bf16[288,288]{1,0:T(8,128)(2,1)S(1)}, bf16[72,144]{1,0:T(8,128)(2,1)S(1)}, bf16[72,144]{1,0:T(8,128)(2,1)S(...) custom-call(bf16[2,144,512]{2,1,0:T(8,128)(2,1)} %bitcast.19, ...), custom_call_target="tpu_custom_call" | custom-call | tf_op jit(solution)/shard_map/load/pallas_call | solution.py:69
  29.4 0.1 pad_add_fusion.lev_ref.place_ref
  29.5 0.0 collective-permute-done.1.second_ref
  29.5 8.5 %collective-permute-done.first_ref = bf16[2,72,512]{2,1,0:T(8,128)(2,1)S(1)} collective-permute-done((bf16[2,72,512]{2,1,0:T(8,128)(2,1)S(1)}, bf16[2,72,512]{2,1,0:T(8,128)(2,1)S(1)}, u32[]{:S(2)}, u32[]{:S(2)}) %collective-permute-start) | collective-permute-done | bytes 147488 | tf_op jit(solution)/shard_map/ppermute | solution.py:27
  38.0 1.0 %shard_map.145 = (bf16[216,512]{1,0:T(8,128)(2,1)S(1)}, bf16[216,512]{1,0:T(8,128)(2,1)S(1)}, bf16[144,512]{1,0:T(8,128)(2,1)S(1)}, bf16[72,512]{1,0:T(8,128)(2,1)S(1)}) custom-call(s32[4]{0:T(128)S(1)} %pad_add_fusion.lev_ref.place_ref, bf16[288,288]{1,0:T(8,128)(2,1)S(1)} %get-tuple-element.26.pick_ref, ...), custom_call_target="tpu_custom_call" | custom-call | tf_op jit(solution)/shard_map/pallas_call | solution.py:230
  39.0 3.5 %collective-permute-start.2 = (bf16[216,512]{1,0:T(8,128)(2,1)S(1)}, bf16[216,512]{1,0:T(8,128)(2,1)S(1)}, u32[]{:S(2)}, u32[]{:S(2)}) collective-permute-start(bf16[216,512]{1,0:T(8,128)(2,1)S(1)} %get-tuple-element.29.paired_ref), channel_id=1, source_target_pairs={{0,512},{1,513},{2,514},{3,515},{4,516},{5,517},{6,518},{7,519},{8... | collective-permute-start | bytes 663560 | tf_op jit(solution)/shard_map/ppermute | solution.py:27
  42.5 7.4 %collective-permute-start.3 = (bf16[144,512]{1,0:T(8,128)(2,1)S(1)}, bf16[144,512]{1,0:T(8,128)(2,1)S(1)}, u32[]{:S(2)}, u32[]{:S(2)}) collective-permute-start(bf16[144,512]{1,0:T(8,128)(2,1)S(1)} %get-tuple-element.30), channel_id=1, source_target_pairs={{0,15},{1,0},{2,1},{3,2},{4,3},{5,4},{6,5},{7,6},{8,7},{9,8},{10,9... | collective-permute-start | bytes 442376 | tf_op jit(solution)/shard_map/ppermute | solution.py:27
  49.9 2.6 %collective-permute-start.4 = (bf16[72,512]{1,0:T(8,128)(2,1)S(1)}, bf16[72,512]{1,0:T(8,128)(2,1)S(1)}, u32[]{:S(2)}, u32[]{:S(2)}) collective-permute-start(bf16[72,512]{1,0:T(8,128)(2,1)S(1)} %get-tuple-element.31), channel_id=1, source_target_pairs={{0,527},{1,512},{2,513},{3,514},{4,515},{5,516},{6,517},{7,518},{8... | collective-permute-start | bytes 221192 | tf_op jit(solution)/shard_map/ppermute | solution.py:27
  52.5 3.4 %collective-permute-done.4.cross_ref = bf16[72,512]{1,0:T(8,128)(2,1)S(1)} collective-permute-done((bf16[72,512]{1,0:T(8,128)(2,1)S(1)}, bf16[72,512]{1,0:T(8,128)(2,1)S(1)}, u32[]{:S(2)}, u32[]{:S(2)}) %collective-permute-start.4) | collective-permute-done | bytes 73760 | tf_op jit(solution)/shard_map/ppermute | solution.py:27
  56.0 0.0 collective-permute-done.3.east_ref
  56.0 0.0 collective-permute-done.2.other_ref
  56.0 4.2 %shard_map.146 = (bf16[144,512]{1,0:T(8,128)(2,1)S(1)}, bf16[72,512]{1,0:T(8,128)(2,1)S(1)}) custom-call(s32[4]{0:T(128)S(1)} %pad_add_fusion.lev_ref.place_ref, bf16[216,512]{1,0:T(8,128)(2,1)S(1)} %get-tuple-element.28.alone_ref, bf16[216,512]{1,0:T(8,128)(2,1)S(1)} %get-tuple-element.29.paired_ref, bf16[216,512]{1,0:T(8,128)(2,1)S(1)} %collective-permute-done.2.other_ref, ...), custom_call_target="tpu_custom_call" | custom-call | tf_op jit(solution)/shard_map/pallas_call | solution.py:230
  60.2 1.9 %collective-permute-start.5 = (bf16[72,512]{1,0:T(8,128)(2,1)S(1)}, bf16[72,512]{1,0:T(8,128)(2,1)S(1)}, u32[]{:S(2)}, u32[]{:S(2)}) collective-permute-start(bf16[72,512]{1,0:T(8,128)(2,1)S(1)} %get-tuple-element.45), channel_id=1, source_target_pairs={{0,1},{1,2},{2,3},{3,4},{4,5},{5,6},{6,7},{7,8},{8,9},{9,10},{10,1... | collective-permute-start | bytes 221192 | tf_op jit(solution)/shard_map/ppermute | solution.py:27
  62.1 4.3 %shard_map.147.partial_ref = bf16[2,144,512]{2,1,0:T(8,128)(2,1)S(1)} custom-call(s32[4]{0:T(128)S(1)} %pad_add_fusion.lev_ref.place_ref, bf16[216,512]{1,0:T(8,128)(2,1)S(1)} %get-tuple-element.28.alone_ref, bf16[216,512]{1,0:T(8,128)(2,1)S(1)} %get-tuple-element.29.paired_ref, bf16[216,512]{1,0:T(8,128)(2,1)S(1)} %collective-permute-done.2.other_ref, ...), custom_call_target="tpu_custom_call" | custom-call | tf_op jit(solution)/shard_map/pallas_call | solution.py:230
  66.5 3.1 %collective-permute-done.5.returned_ref = bf16[72,512]{1,0:T(8,128)(2,1)S(1)} collective-permute-done((bf16[72,512]{1,0:T(8,128)(2,1)S(1)}, bf16[72,512]{1,0:T(8,128)(2,1)S(1)}, u32[]{:S(2)}, u32[]{:S(2)}) %collective-permute-start.5) | collective-permute-done | bytes 73760 | tf_op jit(solution)/shard_map/ppermute | solution.py:27
  69.6 1.5 %shard_map.148 = bf16[2,144,512]{2,1,0:T(8,128)(2,1)} custom-call(s32[4]{0:T(128)S(1)} %pad_add_fusion.lev_ref.place_ref, bf16[2,144,512]{2,1,0:T(8,128)(2,1)S(1)} %shard_map.147.partial_ref, bf16[72,512]{1,0:T(8,128)(2,1)S(1)} %collective-permute-done.5.returned_ref, bf16[288,72]{1,0:T(8,128)(2,1)S(1)} %get-tuple-element.46.returned_to_ref), custom_call_target="tpu_custom_call" | custom-call | tf_op jit(solution)/shard_map/pallas_call | solution.py:230
Async XLA Ops:
  1.0 28.5 %collective-permute-start.1 = (bf16[2,72,512]{2,1,0:T(8,128)(2,1)S(1)}, bf16[2,72,512]{2,1,0:T(8,128)(2,1)S(1)}, u32[]{:S(2)}, u32[]{:S(2)}) collective-permute-start(bf16[2,72,512]{2,1,0:T(8,128)(2,1)S(1)} %get-tuple-element.47), channel_id=1, source_target_pairs={{0,16},{1,17},{2,18},{3,19},{4,20},{5,21},{6,22},{7,23},{8,24},{9,... | collective-permute-start | bytes 442376 | tf_op jit(solution)/shard_map/ppermute | solution.py:27
  12.5 25.5 %collective-permute-start = (bf16[2,72,512]{2,1,0:T(8,128)(2,1)S(1)}, bf16[2,72,512]{2,1,0:T(8,128)(2,1)S(1)}, u32[]{:S(2)}, u32[]{:S(2)}) collective-permute-start(bf16[2,72,512]{2,1,0:T(8,128)(2,1)S(1)} %get-tuple-element.48), channel_id=1, source_target_pairs={{0,496},{1,497},{2,498},{3,499},{4,500},{5,501},{6,502},{7,503},{8... | collective-permute-start | bytes 442376 | tf_op jit(solution)/shard_map/ppermute | solution.py:27
  39.0 17.0 %collective-permute-start.2 = (bf16[216,512]{1,0:T(8,128)(2,1)S(1)}, bf16[216,512]{1,0:T(8,128)(2,1)S(1)}, u32[]{:S(2)}, u32[]{:S(2)}) collective-permute-start(bf16[216,512]{1,0:T(8,128)(2,1)S(1)} %get-tuple-element.29.paired_ref), channel_id=1, source_target_pairs={{0,512},{1,513},{2,514},{3,515},{4,516},{5,517},{6,518},{7,519},{8... | collective-permute-start | bytes 663560 | tf_op jit(solution)/shard_map/ppermute | solution.py:27
  42.5 13.5 %collective-permute-start.3 = (bf16[144,512]{1,0:T(8,128)(2,1)S(1)}, bf16[144,512]{1,0:T(8,128)(2,1)S(1)}, u32[]{:S(2)}, u32[]{:S(2)}) collective-permute-start(bf16[144,512]{1,0:T(8,128)(2,1)S(1)} %get-tuple-element.30), channel_id=1, source_target_pairs={{0,15},{1,0},{2,1},{3,2},{4,3},{5,4},{6,5},{7,6},{8,7},{9,8},{10,9... | collective-permute-start | bytes 442376 | tf_op jit(solution)/shard_map/ppermute | solution.py:27
  49.9 6.1 %collective-permute-start.4 = (bf16[72,512]{1,0:T(8,128)(2,1)S(1)}, bf16[72,512]{1,0:T(8,128)(2,1)S(1)}, u32[]{:S(2)}, u32[]{:S(2)}) collective-permute-start(bf16[72,512]{1,0:T(8,128)(2,1)S(1)} %get-tuple-element.31), channel_id=1, source_target_pairs={{0,527},{1,512},{2,513},{3,514},{4,515},{5,516},{6,517},{7,518},{8... | collective-permute-start | bytes 221192 | tf_op jit(solution)/shard_map/ppermute | solution.py:27
  60.2 9.3 %collective-permute-start.5 = (bf16[72,512]{1,0:T(8,128)(2,1)S(1)}, bf16[72,512]{1,0:T(8,128)(2,1)S(1)}, u32[]{:S(2)}, u32[]{:S(2)}) collective-permute-start(bf16[72,512]{1,0:T(8,128)(2,1)S(1)} %get-tuple-element.45), channel_id=1, source_target_pairs={{0,1},{1,2},{2,3},{3,4},{4,5},{5,6},{6,7},{7,8},{8,9},{9,10},{10,1... | collective-permute-start | bytes 221192 | tf_op jit(solution)/shard_map/ppermute | solution.py:27

commit v5 on v4

--- a/solution.py
+++ b/solution.py
@@ -41,18 +41,26 @@
     return jnp.asarray(table, jnp.bfloat16)
 
 
-def gather_kernel(lev_ref, pick_ref, own_ref, first_ref, second_ref, alone_ref, paired_ref, west_ref, cross_ref):
-    lev = lev_ref[0]
-    kept = alone_ref.shape[0]
-    edge = cross_ref.shape[0]
+def edge_rows(place_ref, which, kept, edge):
+    odd = place_ref[4]
+    return pl.ds(pl.multiple_of(kept + edge * (odd if which == 0 else 1 - odd), 8), edge)
+
+
+def gather_kernel(
+    place_ref, pick_ref, own_ref, first_ref, second_ref,
+    alone_ref, paired_ref, swap_1_ref, swap_2_ref, cross_1_ref, cross_2_ref,
+):
+    lev = place_ref[0]
+    edge = cross_1_ref.shape[0]
+    kept = alone_ref.shape[0] - 2 * edge
     for i, (level, out_ref) in enumerate(((lev, alone_ref), (1 - lev, paired_ref))):
         source = jnp.concatenate([own_ref[level], first_ref[level], second_ref[level]], 0)
         picked = jnp.dot(pick_ref[...], source, preferred_element_type=jnp.float32)
-        picked = picked.astype(jnp.bfloat16)
-        out_ref[...] = picked[:kept]
-        west_ref[i * edge : (i + 1) * edge, :] = picked[kept:]
-        if i == 1:
-            cross_ref[...] = picked[kept:]
+        out_ref[...] = picked.astype(jnp.bfloat16)
+        for which, swap_ref in enumerate((swap_1_ref, swap_2_ref)):
+            swap_ref[i * edge : (i + 1) * edge, :] = out_ref[edge_rows(place_ref, which, kept, edge), :]
+    for which, cross_ref in enumerate((cross_1_ref, cross_2_ref)):
+        cross_ref[...] = paired_ref[edge_rows(place_ref, which, kept, edge), :]
 
 
 def load_kernel(*refs):
@@ -128,30 +136,32 @@
     return jnp.concatenate(parts, 1)
 
 
-def allowed_keys(place_ref, queries, group):
+def allowed_keys(place_ref, queries, keys, group, sets):
     first = place_ref[3]
-    shape = (queries, 2 * queries)
+    shape = (queries, keys)
     row = lax.broadcasted_iota(jnp.int32, shape, 0)
     col = lax.broadcasted_iota(jnp.int32, shape, 1)
+    q_set = row // group
+    k_set = lax.rem(col // (2 * group), sets)
     row = lax.rem(row, group)
     col = lax.rem(col, 2 * group)
     quarter = group // 2
     q_half = jnp.where(row < quarter, 0, 1)
     k_half = jnp.where(col < quarter, 0, jnp.where(col < 2 * quarter, 1, jnp.where(col < 3 * quarter, first, 1 - first)))
     closed = jnp.where(k_half == 0, place_ref[1], place_ref[2])
-    return jnp.where((q_half == k_half) & ((col < group) | (closed == 0)), 1.0, 0.0)
-
-
-def run_windows(sources, query, place_ref, group, heads_ref, logit_ref, weights, kv_ref):
+    return jnp.where((q_half == k_half) & (q_set == k_set) & ((col < group) | (closed == 0)), 1.0, 0.0)
+
+
+def run_windows(sources, query, place_ref, group, sets, heads_ref, logit_ref, weights, kv_ref):
     qkv_ref, proj_ref, up_ref, down_ref, gain_attn_ref, gain_mlp_ref = weights
     width = proj_ref.shape[0]
     tokens = kv_ref.shape[0]
     span = tokens // 3
-    count = span // 2
+    count = query.shape[0] // 2
     kv = jnp.dot(sources, qkv_ref[:, width:], preferred_element_type=jnp.float32)
     kv_ref[...] = kv.astype(jnp.bfloat16)
     q = jnp.dot(query, qkv_ref[:, :width], preferred_element_type=jnp.float32).astype(jnp.bfloat16)
-    own = allowed_keys(place_ref, count, group)
+    own = allowed_keys(place_ref, count, span, group, sets)
     logit = logit_ref[...] * LOG2E
     mixed = []
     for i, (first, last, allowed) in enumerate(((0, span, own), (span, tokens, jnp.concatenate([own, own], 1)))):
@@ -169,56 +179,46 @@
     return result.astype(jnp.bfloat16)
 
 
-def border_kernel(
-    place_ref, alone_ref, paired_ref, other_ref, east_ref, cross_ref, pick_ref, back_ref, heads_ref, logit_ref,
-    qkv_ref, proj_ref, up_ref, down_ref, gain_attn_ref, gain_mlp_ref, out_ref, return_ref, kv_ref,
-):
-    edge = cross_ref.shape[0]
-    start = alone_ref.shape[0] - edge
-    pieces = (
-        alone_ref[start:, :], east_ref[:edge, :], paired_ref[start:, :], east_ref[edge:, :],
-        other_ref[start:, :], cross_ref[...],
-    )
-    sources = jnp.concatenate(pieces, 0)
-    query = [
-        jnp.dot(pick_ref[...], sources[i * 2 * edge : (i + 1) * 2 * edge], preferred_element_type=jnp.float32)
-        for i in range(2)
-    ]
-    query = jnp.concatenate(query, 0).astype(jnp.bfloat16)
-    weights = (qkv_ref, proj_ref, up_ref, down_ref, gain_attn_ref, gain_mlp_ref)
-    result = run_windows(sources, query, place_ref, edge // 2, heads_ref, logit_ref, weights, kv_ref)
-    out_ref[...] = result
-    back = jnp.dot(back_ref[...], result, preferred_element_type=jnp.float32)
-    return_ref[...] = back.astype(jnp.bfloat16)
-
-
 def middle_kernel(
-    place_ref, alone_ref, paired_ref, other_ref, border_ref, middle_to_ref, border_to_ref, heads_ref, logit_ref,
+    place_ref, alone_ref, paired_ref, other_ref, heads_ref, logit_ref,
     qkv_ref, proj_ref, up_ref, down_ref, gain_attn_ref, gain_mlp_ref, out_ref, kv_ref,
 ):
-    lev = place_ref[0]
     span = kv_ref.shape[0] // 3
     count = span // 2
     sources = jnp.concatenate([alone_ref[:span, :], paired_ref[:span, :], other_ref[:span, :]], 0)
     query = jnp.concatenate([alone_ref[:count, :], paired_ref[:count, :]], 0)
     weights = (qkv_ref, proj_ref, up_ref, down_ref, gain_attn_ref, gain_mlp_ref)
-    result = run_windows(sources, query, place_ref, count, heads_ref, logit_ref, weights, kv_ref)
+    out_ref[...] = run_windows(sources, query, place_ref, count, 1, heads_ref, logit_ref, weights, kv_ref)
+
+
+def border_kernel(
+    place_ref, alone_ref, paired_ref, other_ref, swap_1_ref, swap_2_ref, cross_1_ref, cross_2_ref, middle_ref,
+    pick_ref, middle_to_ref, border_to_ref, heads_ref, logit_ref,
+    qkv_ref, proj_ref, up_ref, down_ref, gain_attn_ref, gain_mlp_ref, out_ref, kv_ref,
+):
+    lev = place_ref[0]
+    edge = cross_1_ref.shape[0]
+    kept = alone_ref.shape[0] - 2 * edge
+    pieces = []
+    for i, ref in enumerate((alone_ref, paired_ref, other_ref)):
+        pieces += [ref[edge_rows(place_ref, which, kept, edge), :] for which in range(2)]
+        if i < 2:
+            pieces += [swap[i * edge : (i + 1) * edge, :] for swap in (swap_1_ref, swap_2_ref)]
+        else:
+            pieces += [cross_1_ref[...], cross_2_ref[...]]
+    sources = jnp.concatenate(pieces, 0)
+    query = [
+        jnp.dot(pick_ref[...], sources[i * 4 * edge : i * 4 * edge + 2 * edge], preferred_element_type=jnp.float32)
+        for i in range(2)
+    ]
+    query = jnp.concatenate(query, 0).astype(jnp.bfloat16)
+    weights = (qkv_ref, proj_ref, up_ref, down_ref, gain_attn_ref, gain_mlp_ref)
+    result = run_windows(sources, query, place_ref, edge // 2, 2, heads_ref, logit_ref, weights, kv_ref)
+    border_to = border_to_ref[place_ref[4]]
     for i, level in enumerate((lev, 1 - lev)):
-        placed = jnp.dot(middle_to_ref[...], result[i * count : (i + 1) * count], preferred_element_type=jnp.float32)
-        placed += jnp.dot(border_to_ref[...], border_ref[i * count : (i + 1) * count, :], preferred_element_type=jnp.float32)
+        placed = jnp.dot(middle_to_ref[...], middle_ref[i * edge : (i + 1) * edge, :], preferred_element_type=jnp.float32)
+        placed += jnp.dot(border_to, result[i * edge : (i + 1) * edge], preferred_element_type=jnp.float32)
         out_ref[level] = placed.astype(jnp.bfloat16)
-
-
-def place_kernel(place_ref, partial_ref, returned_ref, returned_to_ref, out_ref):
-    lev = place_ref[0]
-    own = partial_ref.shape[1]
-    for i, level in enumerate((lev, 1 - lev)):
-        placed = jnp.dot(
-            returned_to_ref[i * own : (i + 1) * own, :], returned_ref[...], preferred_element_type=jnp.float32
-        )
-        row = lax.broadcasted_iota(jnp.int32, placed.shape, 0)
-        mine = lax.rem(row, own // WA) >= EDGE
-        out_ref[level] = jnp.where(mine, partial_ref[level], placed.astype(jnp.bfloat16))
 
 
 VMEM = pl.BlockSpec(memory_space=pltpu.VMEM)
@@ -253,48 +253,51 @@
     lev = lax.axis_index("lev").astype(jnp.int32)
     lat = lax.axis_index("lat")
     last = lax.axis_size("lat") - 1
-    place = jnp.stack([lev, (lat == 0).astype(jnp.int32), (lat == last).astype(jnp.int32), lax.rem(lat, 2).astype(jnp.int32)])
+    place = jnp.stack([lev, (lat == 0).astype(jnp.int32), (lat == last).astype(jnp.int32), 1 - lax.rem(lat, 2).astype(jnp.int32), lax.rem(lax.axis_index("lon"), 2).astype(jnp.int32)])
 
     tokens = grid.reshape(levels, own, width)
     halves = grid.reshape(levels, 2, half, width)
-    odd = lax.rem(lat, 2).astype(jnp.int32)
-    sent_first = lax.dynamic_index_in_dim(halves, odd, 1, keepdims=False)
-    sent_second = lax.dynamic_index_in_dim(halves, 1 - odd, 1, keepdims=False)
-    first = send(sent_first, lambda c, i, j: (c, i - 1 + 2 * (i % 2), j))
-    second = send(sent_second, lambda c, i, j: (c, i + 1 - 2 * (i % 2), j))
+    even = 1 - lax.rem(lat, 2).astype(jnp.int32)
+    sent_first = lax.dynamic_index_in_dim(halves, even, 1, keepdims=False)
+    sent_second = lax.dynamic_index_in_dim(halves, 1 - even, 1, keepdims=False)
+    first = send(sent_first, lambda c, i, j: (c, i + 1 - 2 * (i % 2), j))
+    second = send(sent_second, lambda c, i, j: (c, i - 1 + 2 * (i % 2), j))
 
     groups = column_group(cols, EDGE, EDGE + WO) + column_group(cols, EDGE + WO, cols) + column_group(cols, 0, EDGE)
     heads_of = jnp.asarray(np.repeat(np.eye(heads, dtype=np.float32), width // heads, axis=1), bf16)
     quarter = edge // 2
     spots = [(r, c) for r in range(rows) for c in range(cols)]
-    pick = [edge + t for t in range(quarter)] + list(range(quarter))
-    back = [i * edge + t for i in range(2) for t in range(quarter)]
+    pick = list(range(quarter)) + [edge + t for t in range(quarter)]
     middle_to = [r * WO + c - EDGE if EDGE <= c < EDGE + WO else -1 for r, c in spots]
-    border_to = [quarter + r * EDGE + c - EDGE - WO if c >= EDGE + WO else -1 for r, c in spots]
-    returned_to = [i * quarter + r * EDGE + c if c < EDGE else -1 for i in range(2) for r, c in spots]
-    tokens, groups, pick, back, middle_to, border_to, returned_to, *shared = load(
-        tokens, one_hot(groups, 2 * own), one_hot(pick, 2 * edge), one_hot(back, 2 * edge), one_hot(middle_to, edge),
-        one_hot(border_to, edge), one_hot(returned_to, edge),
+
+    def edge_spot(odd, r, c):
+        if EDGE <= c < EDGE + WO:
+            return -1
+        west = c < EDGE
+        return quarter * (west != odd) + r * EDGE + (c if west else c - EDGE - WO)
+
+    border_to = [one_hot([edge_spot(odd, r, c) for r, c in spots], edge) for odd in (False, True)]
+    tokens, groups, pick, middle_to, border_to, *shared = load(
+        tokens, one_hot(groups, 2 * own), one_hot(pick, 2 * edge), one_hot(middle_to, edge), jnp.stack(border_to),
         heads_of, logit_scale.reshape(1, heads), w_qkv, w_proj, w_up, w_down,
         gain_attn.reshape(1, width), gain_mlp.reshape(1, width),
     )
 
-    kept = 2 * own - edge
-    outs = (shape(kept, width), shape(kept, width), shape(2 * edge, width), shape(edge, width))
-    alone, paired, west, west_paired = call(gather_kernel, outs, 8)(place, groups, tokens, first, second)
-    east = send(west, lambda c, i, j: (c, i, j - 1))
-    cross = send(west_paired, lambda c, i, j: (1 - c, i, j - 1))
+    both = shape(2 * edge, width)
+    outs = (shape(2 * own, width), shape(2 * own, width), both, both, shape(edge, width), shape(edge, width))
+    alone, paired, swap_1, swap_2, cross_1, cross_2 = call(gather_kernel, outs, 8)(place, groups, tokens, first, second)
+    swap_1 = send(swap_1, lambda c, i, j: (c, i, j + 1 - 2 * (j % 2)))
+    swap_2 = send(swap_2, lambda c, i, j: (c, i, j - 1 + 2 * (j % 2)))
     other = send(paired, lambda c, i, j: (1 - c, i, j))
+    cross_1 = send(cross_1, lambda c, i, j: (1 - c, i, j + 1 - 2 * (j % 2)))
+    cross_2 = send(cross_2, lambda c, i, j: (1 - c, i, j - 1 + 2 * (j % 2)))
 
     kv = [pltpu.VMEM((6 * edge, 2 * width), bf16)]
-    border, returning = call(border_kernel, (shape(2 * edge, width), shape(edge, width)), 16, kv)(
-        place, alone, paired, other, east, cross, pick, back, *shared
+    middle = call(middle_kernel, both, 16, kv)(place, alone, paired, other, *shared)
+    kv = [pltpu.VMEM((12 * edge, 2 * width), bf16)]
+    out = call(border_kernel, shape(levels, own, width), 20, kv)(
+        place, alone, paired, other, swap_1, swap_2, cross_1, cross_2, middle, pick, middle_to, border_to, *shared
     )
-    returned = send(returning, lambda c, i, j: (c, i, j + 1))
-    partial = call(middle_kernel, shape(levels, own, width), 16, kv)(
-        place, alone, paired, other, border, middle_to, border_to, *shared
-    )
-    out = call(place_kernel, shape(levels, own, width), 8)(place, partial, returned, returned_to)
     return out.reshape(levels, rows, cols, width)
 
 

time: 71.3 us -> 72.6 us (1.018)
  starting transfers between devices: 40.4 us -> 48.6 us
  waiting for transfers between devices: 15 us -> 8.2 us
    ppermute x6 -> x7, starting transfers between devices: 40.4 us -> 48.6 us  [send(): return lax.ppermute(array, AXES, route)]
    ppermute x6 -> x7, waiting for transfers between devices: 15 us -> 8.2 us  [send(): return lax.ppermute(array, AXES, route)]
    pallas_call x4 -> x3, Pallas kernels: 11 us -> 11 us  [run(): pl.pallas_call(kernel, out_shape=outs, in_specs=[SMEM] + [VMEM] * len(arg...]
  transfers between devices with their start and end apart: 6 -> 7, of which waited for: 3 -> 3; matrix products, arithmetic and copies ran while one was open for 0% -> 0% of each run, Pallas kernels for 11% -> 10%
where the time goes in v5:
time: 72.6 us; the launch traced here: 72.3 us
  starting transfers between devices  48.6 us (67%)
  Pallas kernels  14.3 us (20%)
  waiting for transfers between devices  8.2 us (11%)
  local copies, waits for them, and re-layouts  1.09 us (2%)
    ppermute x7, starting transfers between devices, send(): return lax.ppermute(array, AXES, route)  48.6 us
    pallas_call x3, Pallas kernels, run(): pl.pallas_call(kernel, out_shape=outs, in_specs=[SMEM] + [VMEM] * len(arg...  11 us
    ppermute x7, waiting for transfers between devices, send(): return lax.ppermute(array, AXES, route)  8.2 us
    pallas_call x1, Pallas kernels, load(): pl.pallas_call(load_kernel, out_shape=tuple((jax.ShapeDtypeStruct(a.shape...  3.3 us
  transfers between devices with their start and end apart: 7, of which 3 were waited for; matrix products, arithmetic and copies ran while one was open for 0% of the time, Pallas kernels for 10%

profile of v5, /device:TPU:1, one launch (start us, length us, event | category | flops | bytes accessed | tf_op | source)
XLA Modules:
  0.0 72.3 jit_solution(16983684327466929102)
XLA Ops:
  0.0 1.0 %dynamic-slice_bitcast_fusion = (bf16[2,72,512]{2,1,0:T(8,128)(2,1)S(1)}, bf16[2,72,512]{2,1,0:T(8,128)(2,1)S(1)}) fusion(bf16[2,2,72,512]{3,2,1,0:T(8,128)(2,1)} %bitcast.19, s32[]{:T(128)S(6)} %select_n.8, s32[]{:T(128)S(6)} %select_n.7), kind=kLoop, calls=%fused_computation | loop fusion | bytes 589832 | tf_op jit(solution)/shard_map/jit(dynamic_index_in_dim)/squeeze | solution.py:262
  1.0 21.6 %collective-permute-start.1 = (bf16[2,72,512]{2,1,0:T(8,128)(2,1)S(1)}, bf16[2,72,512]{2,1,0:T(8,128)(2,1)S(1)}, u32[]{:S(2)}, u32[]{:S(2)}) collective-permute-start(bf16[2,72,512]{2,1,0:T(8,128)(2,1)S(1)} %get-tuple-element.43), channel_id=1, source_target_pairs={{0,496},{1,497},{2,498},{3,499},{4,500},{5,501},{6,502},{7,503},{8... | collective-permute-start | bytes 442376 | tf_op jit(solution)/shard_map/ppermute | solution.py:27
  22.6 1.9 %collective-permute-start = (bf16[2,72,512]{2,1,0:T(8,128)(2,1)S(1)}, bf16[2,72,512]{2,1,0:T(8,128)(2,1)S(1)}, u32[]{:S(2)}, u32[]{:S(2)}) collective-permute-start(bf16[2,72,512]{2,1,0:T(8,128)(2,1)S(1)} %get-tuple-element.44), channel_id=1, source_target_pairs={{0,16},{1,17},{2,18},{3,19},{4,20},{5,21},{6,22},{7,23},{8,24},{9,... | collective-permute-start | bytes 442376 | tf_op jit(solution)/shard_map/ppermute | solution.py:27
  24.6 0.1 stack.40.place_ref
  24.7 3.3 %load.1 = (bf16[2,144,512]{2,1,0:T(8,128)(2,1)S(1)}, bf16[288,288]{1,0:T(8,128)(2,1)S(1)}, bf16[72,144]{1,0:T(8,128)(2,1)S(1)}, bf16[144,72]{1,0:T(8,128)(2,1)S(...) custom-call(bf16[2,144,512]{2,1,0:T(8,128)(2,1)} %bitcast.20, ...), custom_call_target="tpu_custom_call" | custom-call | tf_op jit(solution)/shard_map/load/pallas_call | solution.py:77
  28.0 3.4 %collective-permute-done.1.second_ref = bf16[2,72,512]{2,1,0:T(8,128)(2,1)S(1)} collective-permute-done((bf16[2,72,512]{2,1,0:T(8,128)(2,1)S(1)}, bf16[2,72,512]{2,1,0:T(8,128)(2,1)S(1)}, u32[]{:S(2)}, u32[]{:S(2)}) %collective-permute-start.1) | collective-permute-done | bytes 147488 | tf_op jit(solution)/shard_map/ppermute | solution.py:27
  31.4 4.4 %collective-permute-done.first_ref = bf16[2,72,512]{2,1,0:T(8,128)(2,1)S(1)} collective-permute-done((bf16[2,72,512]{2,1,0:T(8,128)(2,1)S(1)}, bf16[2,72,512]{2,1,0:T(8,128)(2,1)S(1)}, u32[]{:S(2)}, u32[]{:S(2)}) %collective-permute-start) | collective-permute-done | bytes 147488 | tf_op jit(solution)/shard_map/ppermute | solution.py:27
  35.8 1.0 %shard_map.136 = (bf16[288,512]{1,0:T(8,128)(2,1)S(1)}, bf16[288,512]{1,0:T(8,128)(2,1)S(1)}, bf16[144,512]{1,0:T(8,128)(2,1)S(1)}, bf16[144,512]{1,0:T(8,128)(2...) custom-call(s32[5]{0:T(128)S(1)} %stack.40.place_ref, ...), custom_call_target="tpu_custom_call" | custom-call | tf_op jit(solution)/shard_map/pallas_call | solution.py:230
  36.8 10.4 %collective-permute-start.2 = (bf16[288,512]{1,0:T(8,128)(2,1)S(1)}, bf16[288,512]{1,0:T(8,128)(2,1)S(1)}, u32[]{:S(2)}, u32[]{:S(2)}) collective-permute-start(bf16[288,512]{1,0:T(8,128)(2,1)S(1)} %get-tuple-element.27.paired_ref), channel_id=1, source_target_pairs={{0,512},{1,513},{2,514},{3,515},{4,516},{5,517},{6,518},{7,519},{8... | collective-permute-start | bytes 884744 | tf_op jit(solution)/shard_map/ppermute | solution.py:27
  47.1 3.1 %collective-permute-start.3 = (bf16[144,512]{1,0:T(8,128)(2,1)S(1)}, bf16[144,512]{1,0:T(8,128)(2,1)S(1)}, u32[]{:S(2)}, u32[]{:S(2)}) collective-permute-start(bf16[144,512]{1,0:T(8,128)(2,1)S(1)} %get-tuple-element.28), channel_id=1, source_target_pairs={{0,1},{1,0},{2,3},{3,2},{4,5},{5,4},{6,7},{7,6},{8,9},{9,8},{10,11... | collective-permute-start | bytes 442376 | tf_op jit(solution)/shard_map/ppermute | solution.py:27
  50.3 1.9 %collective-permute-start.4 = (bf16[144,512]{1,0:T(8,128)(2,1)S(1)}, bf16[144,512]{1,0:T(8,128)(2,1)S(1)}, u32[]{:S(2)}, u32[]{:S(2)}) collective-permute-start(bf16[144,512]{1,0:T(8,128)(2,1)S(1)} %get-tuple-element.29), channel_id=1, source_target_pairs={{0,15},{1,2},{2,1},{3,4},{4,3},{5,6},{6,5},{7,8},{8,7},{9,10},{10,... | collective-permute-start | bytes 442376 | tf_op jit(solution)/shard_map/ppermute | solution.py:27
  52.2 4.5 %collective-permute-start.5 = (bf16[72,512]{1,0:T(8,128)(2,1)S(1)}, bf16[72,512]{1,0:T(8,128)(2,1)S(1)}, u32[]{:S(2)}, u32[]{:S(2)}) collective-permute-start(bf16[72,512]{1,0:T(8,128)(2,1)S(1)} %get-tuple-element.30), channel_id=1, source_target_pairs={{0,513},{1,512},{2,515},{3,514},{4,517},{5,516},{6,519},{7,518},{8... | collective-permute-start | bytes 221192 | tf_op jit(solution)/shard_map/ppermute | solution.py:27
  56.7 5.2 %collective-permute-start.6 = (bf16[72,512]{1,0:T(8,128)(2,1)S(1)}, bf16[72,512]{1,0:T(8,128)(2,1)S(1)}, u32[]{:S(2)}, u32[]{:S(2)}) collective-permute-start(bf16[72,512]{1,0:T(8,128)(2,1)S(1)} %get-tuple-element.31), channel_id=1, source_target_pairs={{0,527},{1,514},{2,513},{3,516},{4,515},{5,518},{6,517},{7,520},{8... | collective-permute-start | bytes 221192 | tf_op jit(solution)/shard_map/ppermute | solution.py:27
  61.9 0.0 collective-permute-done.2.other_ref
  61.9 4.0 %shard_map.137.middle_ref = bf16[144,512]{1,0:T(8,128)(2,1)S(1)} custom-call(s32[5]{0:T(128)S(1)} %stack.40.place_ref, bf16[288,512]{1,0:T(8,128)(2,1)S(1)} %get-tuple-element.26.alone_ref, bf16[288,512]{1,0:T(8,128)(2,1)S(1)} %get-tuple-element.27.paired_ref, bf16[288,512]{1,0:T(8,128)(2,1)S(1)} %collective-permute-done.2.other_ref, ...), custom_call_target="tpu_custom_call" | custom-call | tf_op jit(solution)/shard_map/pallas_call | solution.py:230
  65.9 0.0 collective-permute-done.5.cross_1_ref
  65.9 0.4 collective-permute-done.6.cross_2_ref
  66.3 0.0 collective-permute-done.3.swap_1_ref
  66.3 0.0 collective-permute-done.4.swap_2_ref
  66.3 6.0 %shard_map.138 = bf16[2,144,512]{2,1,0:T(8,128)(2,1)} custom-call(s32[5]{0:T(128)S(1)} %stack.40.place_ref, bf16[288,512]{1,0:T(8,128)(2,1)S(1)} %get-tuple-element.26.alone_ref, bf16[288,512]{1,0:T(8,128)(2,1)S(1)} %get-tuple-element.27.paired_ref, bf16[288,512]{1,0:T(8,128)(2,1)S(1)} %collective-permute-done.2.other_ref, ...), custom_call_target="tpu_custom_call" | custom-call | tf_op jit(solution)/shard_map/pallas_call | solution.py:230
Async XLA Ops:
  1.0 30.3 %collective-permute-start.1 = (bf16[2,72,512]{2,1,0:T(8,128)(2,1)S(1)}, bf16[2,72,512]{2,1,0:T(8,128)(2,1)S(1)}, u32[]{:S(2)}, u32[]{:S(2)}) collective-permute-start(bf16[2,72,512]{2,1,0:T(8,128)(2,1)S(1)} %get-tuple-element.43), channel_id=1, source_target_pairs={{0,496},{1,497},{2,498},{3,499},{4,500},{5,501},{6,502},{7,503},{8... | collective-permute-start | bytes 442376 | tf_op jit(solution)/shard_map/ppermute | solution.py:27
  22.6 13.1 %collective-permute-start = (bf16[2,72,512]{2,1,0:T(8,128)(2,1)S(1)}, bf16[2,72,512]{2,1,0:T(8,128)(2,1)S(1)}, u32[]{:S(2)}, u32[]{:S(2)}) collective-permute-start(bf16[2,72,512]{2,1,0:T(8,128)(2,1)S(1)} %get-tuple-element.44), channel_id=1, source_target_pairs={{0,16},{1,17},{2,18},{3,19},{4,20},{5,21},{6,22},{7,23},{8,24},{9,... | collective-permute-start | bytes 442376 | tf_op jit(solution)/shard_map/ppermute | solution.py:27
  36.8 25.1 %collective-permute-start.2 = (bf16[288,512]{1,0:T(8,128)(2,1)S(1)}, bf16[288,512]{1,0:T(8,128)(2,1)S(1)}, u32[]{:S(2)}, u32[]{:S(2)}) collective-permute-start(bf16[288,512]{1,0:T(8,128)(2,1)S(1)} %get-tuple-element.27.paired_ref), channel_id=1, source_target_pairs={{0,512},{1,513},{2,514},{3,515},{4,516},{5,517},{6,518},{7,519},{8... | collective-permute-start | bytes 884744 | tf_op jit(solution)/shard_map/ppermute | solution.py:27
  47.1 19.2 %collective-permute-start.3 = (bf16[144,512]{1,0:T(8,128)(2,1)S(1)}, bf16[144,512]{1,0:T(8,128)(2,1)S(1)}, u32[]{:S(2)}, u32[]{:S(2)}) collective-permute-start(bf16[144,512]{1,0:T(8,128)(2,1)S(1)} %get-tuple-element.28), channel_id=1, source_target_pairs={{0,1},{1,0},{2,3},{3,2},{4,5},{5,4},{6,7},{7,6},{8,9},{9,8},{10,11... | collective-permute-start | bytes 442376 | tf_op jit(solution)/shard_map/ppermute | solution.py:27
  50.3 16.1 %collective-permute-start.4 = (bf16[144,512]{1,0:T(8,128)(2,1)S(1)}, bf16[144,512]{1,0:T(8,128)(2,1)S(1)}, u32[]{:S(2)}, u32[]{:S(2)}) collective-permute-start(bf16[144,512]{1,0:T(8,128)(2,1)S(1)} %get-tuple-element.29), channel_id=1, source_target_pairs={{0,15},{1,2},{2,1},{3,4},{4,3},{5,6},{6,5},{7,8},{8,7},{9,10},{10,... | collective-permute-start | bytes 442376 | tf_op jit(solution)/shard_map/ppermute | solution.py:27
  52.2 13.7 %collective-permute-start.5 = (bf16[72,512]{1,0:T(8,128)(2,1)S(1)}, bf16[72,512]{1,0:T(8,128)(2,1)S(1)}, u32[]{:S(2)}, u32[]{:S(2)}) collective-permute-start(bf16[72,512]{1,0:T(8,128)(2,1)S(1)} %get-tuple-element.30), channel_id=1, source_target_pairs={{0,513},{1,512},{2,515},{3,514},{4,517},{5,516},{6,519},{7,518},{8... | collective-permute-start | bytes 221192 | tf_op jit(solution)/shard_map/ppermute | solution.py:27
  56.7 9.6 %collective-permute-start.6 = (bf16[72,512]{1,0:T(8,128)(2,1)S(1)}, bf16[72,512]{1,0:T(8,128)(2,1)S(1)}, u32[]{:S(2)}, u32[]{:S(2)}) collective-permute-start(bf16[72,512]{1,0:T(8,128)(2,1)S(1)} %get-tuple-element.31), channel_id=1, source_target_pairs={{0,527},{1,514},{2,513},{3,516},{4,515},{5,518},{6,517},{7,520},{8... | collective-permute-start | bytes 221192 | tf_op jit(solution)/shard_map/ppermute | solution.py:27
